TPU v7x, 32 devices: a whole 2x2x4 slice. The times are simulated.
32 devices in a mesh: sim: 2 (over y), band: 4 (over z), ord: 4 (over x, core).
Axes of the slice: x: 2, y: 2, z: 4, core: 2. Of those that a mesh axis runs over, the one named last changes fastest.
Arguments:
- alm: bfloat16 [12, 256, 8192], P('sim', 'ord', 'band'), parts along dimension 0, may hold values from -6 to 6
- legendre: bfloat16 [16, 256, 8192], P(None, 'ord', 'band'), may hold values from -0.005859375 to 0.005859375
- order_ids: int32 [256], P('ord'), may hold values from 0 to 8191, as said below
- cycle_number: int32 [16], P('band'), may hold values from 1 to 32767
- src_band: int32 [4096, 1], P(('sim', 'band', 'ord')), parts along dimension 0, may hold values from 0 to 3; in each aligned block of 128 rows (0 to 127, 128 to 255, ...) at most 64 rows name the same one
- src_block: int32 [4096], P(('sim', 'band', 'ord')), parts along dimension 0, may hold values from 0 to 127
- weights: bfloat16 [4096, 128, 128], P(('sim', 'band', 'ord')), parts along dimension 0, may hold values from -0.5 to 0.5
Outputs:
- sky_map: bfloat16 [6, 16, 16384], P('sim', 'band', 'ord'), parts along dimension 0
- lensed: float32 [6, 16, 16384], P('sim', 'band', 'ord'), parts along dimension 0
There are 2 independent parts, one for each index of `sim`. A program takes and returns all parts, laid end to end along the dimension named above; an argument that names none is the same for every part. Nothing has to cross between parts.
Inputs may be any that keep to these rules, and one draw needn't show every extreme that they name: `src_band`: among the blocks of one device at most 64 name the same band, a bound that some block reaches. `order_ids`: distinct values; one of them is 0.
All inputs are finite; a program needn't handle non-finite values.
Results may differ from a plain program's by a relative error of at most 0.0029.
Values may be sent and summed in bfloat16 or wider, within the bound.
No kernel may reach another device: no remote copies, remote signals or barrier semaphores. Data moves between devices by JAX's collectives and lax.ppermute only.
A program may use at most 128 MiB of HBM per device.

v0:
```python
import math

import jax
import jax.numpy as jnp
from jax import lax
from jax.sharding import PartitionSpec as P

NPIX = 16384
BLK = 128


def rotate(coeffs, order_ids, cycle_number):
    parity = (cycle_number % 2).astype(jnp.float32)
    orders = order_ids.astype(jnp.float32)
    angle = math.pi / NPIX * orders[None, :] * parity[:, None]
    cosine = jnp.cos(angle)[:, None, :]
    sine = jnp.sin(angle)[:, None, :]
    factor = jnp.where(order_ids == 0, 1.0, 2.0).astype(jnp.float32)[None, None, :]
    real_part = coeffs[:, 0:3, :]
    imag_part = coeffs[:, 3:6, :]
    rot_re = factor * (real_part * cosine - imag_part * sine)
    rot_im = factor * (real_part * sine + imag_part * cosine)
    return (rot_re, rot_im)


def synthesize(rot_re, rot_im, order_ids, columns):
    phase = order_ids[:, None] * columns[None, :] % NPIX
    angle = phase.astype(jnp.float32) * (2.0 * math.pi / NPIX)
    right = jnp.concatenate([jnp.cos(angle), jnp.sin(angle)], axis=0)
    cycles = rot_re.shape[0]
    left = jnp.concatenate([rot_re, -rot_im], axis=2).reshape(cycles * 3, -1)
    pixels = jnp.dot(
        left, right, precision=lax.Precision.HIGHEST, preferred_element_type=jnp.float32
    )
    return jnp.transpose(pixels.reshape(cycles, 3, -1), (1, 0, 2))


def local(alm, legendre, order_ids, cycle_number, src_band, src_block, weights):
    cycles_here = cycle_number.shape[0]
    orders_here = order_ids.shape[0]
    npix_here = NPIX // lax.axis_size("ord")
    part = jnp.einsum("rml,cml->rcm", legendre, alm, preferred_element_type=jnp.float32)
    coeffs = lax.psum_scatter(
        part.reshape(cycles_here * lax.axis_size("band"), 6 * orders_here),
        "band",
        scatter_dimension=0,
        tiled=True,
    )
    coeffs = coeffs.reshape(cycles_here, 6, orders_here)
    all_coeffs, all_orders = (
        lax.all_gather(coeffs, "ord", axis=2, tiled=True),
        lax.all_gather(order_ids, "ord", axis=0, tiled=True),
    )
    rot_re, rot_im = rotate(all_coeffs, all_orders, cycle_number)
    columns = lax.axis_index("ord") * npix_here + jnp.arange(npix_here, dtype=jnp.int32)
    sky_map = synthesize(rot_re, rot_im, all_orders, columns).astype(jnp.bfloat16)
    blocks = sky_map.reshape(3, -1, BLK)
    count_blocks = blocks.shape[1]
    bands = lax.axis_size("band")
    capacity = max(2, 2 * count_blocks // bands)
    target = src_band[:, 0]
    onehot = (target[:, None] == jnp.arange(bands, dtype=jnp.int32)[None, :]).astype(jnp.int32)
    before = jnp.cumsum(onehot, axis=0) - onehot
    position = jnp.sum(before * onehot, axis=1)
    slot_index = target * capacity + position
    requests = jnp.full((bands * capacity,), -1, jnp.int32).at[slot_index].set(src_block)
    requests = requests.reshape(bands, capacity)
    picked = blocks[
        :,
        jnp.clip(
            lax.all_to_all(requests, "band", split_axis=0, concat_axis=0, tiled=True),
            0,
            count_blocks - 1,
        ),
        :,
    ]
    received = lax.all_to_all(picked, "band", split_axis=1, concat_axis=1, tiled=True)
    source = received.reshape(3, bands * capacity, BLK)[:, slot_index, :]
    lensed = jnp.einsum("kij,ckj->cki", weights, source, preferred_element_type=jnp.float32)
    return (sky_map, lensed.reshape(3, cycles_here, npix_here))


def solution(mesh):
    placed = (
        P("sim", "ord", "band"),
        P(None, "ord", "band"),
        P("ord"),
        P("band"),
        P(("sim", "band", "ord"), None),
        P(("sim", "band", "ord")),
        P(("sim", "band", "ord"), None, None),
    )
    return jax.shard_map(
        local,
        mesh=mesh,
        in_specs=placed,
        out_specs=(P("sim", "band", "ord"), P("sim", "band", "ord")),
        check_vma=False,
    )
```

profile of v0, /device:TPU:0, one launch (start us, length us, event | category | flops | bytes accessed | tf_op | source)
XLA Modules:
  0.0 94.6 jit_solution(5537024923657637827)
XLA Ops:
  0.6 0.7 fusion.19
  1.4 0.2 reduce_window_sum.11
  1.5 0.8 select_reduce_fusion
  2.4 0.7 fusion.25
  3.0 1.1 %scatter_custom_fusion = s32[256]{0:T(256)S(1)} fusion(s32[128]{0:T(128)S(1)} %fusion.25, s32[128]{0:T(128)} %param.12, s32[]{:T(128)} %constant.56.clone.1), kind=kCustom, calls=%fused_computation.52 | custom fusion | bytes 1536 | tf_op jit(solution)/shard_map/scatter | solution.py:66
  4.2 0.7 all_to_all.9
  4.8 6.3 %all-to-all-start = ((s32[4,1,64]{2,1,0:T(1,128)}), s32[4,1,64]{2,1,0:T(1,128)S(1)}, u32[]{:S(2)}, u32[]{:S(2)}) async-start(s32[4,1,64]{2,1,0:T(1,128)} %all_to_all.9), calls=%async_computation | async-start | bytes 4096 | tf_op jit(solution)/shard_map/all_to_all | solution.py:71
  11.2 1.2 %dynamic-slice = u32[1]{0:T(128)} dynamic-slice(u32[32]{0:T(128)} %constant.63, u32[]{:T(128)S(6)} %add.58), dynamic_slice_sizes={1} | dynamic-slice | bytes 12
  13.1 0.9 dynamic-update-slice
  13.9 4.9 %all-reduce = s32[256]{0:T(256)S(1)} all-reduce(s32[256]{0:T(256)S(1)} %dynamic-update-slice), channel_id=1, replica_groups=mesh['sim'=2,'band'=4,'ord'=4] {'ord'}, use_global_device_ids=true, to_apply=%add | all-reduce | flops 256 | bytes 2048
  18.8 0.7 fusion.23
  19.5 5.8 %fusion.13 = f32[16,6,64]{0,1,2:T(8,128)S(1)} fusion(bf16[16,64,2048]{2,1,0:T(8,128)(2,1)} %param.8, bf16[6,64,2048]{2,1,0:T(8,128)(2,1)} %param.7), kind=kOutput, calls=%fused_computation.23 | convolution fusion | flops 25165824 | bytes 5791744 | tf_op jit(solution)/shard_map/rml,cml->rcm/dot_general | solution.py:42
  25.3 0.1 copy.19
  25.5 19.4 %all-reduce.1 = f32[16,384]{1,0:T(8,128)S(1)} all-reduce(f32[16,384]{1,0:T(8,128)S(1)} %reshape.100), channel_id=2, replica_groups=mesh['sim'=2,'band'=4,'ord'=4] {'band'}, use_global_device_ids=true, to_apply=%region_0.0.clone | all-reduce | flops 6144 | bytes 49152
  44.9 0.6 dynamic-slice.1
  46.3 0.1 copy.20
  46.4 6.7 %all_gather.7 = f32[4,6,256]{1,0,2:T(4,128)S(1)} all-gather(f32[4,6,64]{1,0,2:T(4,128)S(1)} %copy.20), channel_id=1, replica_groups=mesh['sim'=2,'band'=4,'ord'=4] {'ord'}, dimensions={2}, use_global_device_ids=true | all-gather | bytes 30720 | tf_op jit(solution)/shard_map/all_gather | solution.py:51
  53.1 0.3 fusion.29
  53.5 0.2 copy.27
  53.7 0.2 copy.28
  53.9 16.6 %fusion.12 = (f32[256,4096]{1,0:T(8,128)S(1)}, f32[256,4096]{1,0:T(8,128)S(1)}) fusion(s32[4096]{0:T(1024)S(1)} %iota_add_fusion, s32[256]{0:T(256)S(1)} %all-reduce), kind=kLoop, calls=%fused_computation.21 | loop fusion | flops 14680064 | bytes 8406016 | tf_op jit(solution)/shard_map/cos | solution.py:29
  70.5 0.1 multiply_cosine_fusion
  70.6 4.2 %fusion.4 = bf16[3,4,4096]{2,1,0:T(4,128)(2,1)S(1)} fusion(f32[256,4096]{1,0:T(8,128)S(1)} %get-tuple-element.7, f32[256,4096]{1,0:T(8,128)S(1)} %get-tuple-element.6, f32[4,3,256]{2,0,1:T(4,128)S(1)} %get-tuple-element.5, f32[4,3,256]{2,0,1:T(4,128)S(1)} %get-tuple-element.4), kind=kOutput, calls=%fused_computation.13 | convolution fusion | flops 304142336 | bytes 8511488 | tf_op jit(solution)/shard_map/dot_general | solution.py:32
  74.8 0.1 reshape.102
  75.2 1.0 %gather_fusion = bf16[256,3,128]{2,1,0:T(4,128)(2,1)S(1)} fusion(bf16[3,128,128]{2,0,1:T(4,128)(2,1)S(1)} %copy.23, s32[1024]{0:T(1024)S(1)} %pad_clamp_fusion.1), kind=kCustom, calls=%fused_computation | custom fusion | bytes 394240 | tf_op jit(solution)/shard_map/gather | solution.py:68
  76.1 0.7 copy.38
  76.9 3.4 %all-to-all-start.1 = ((bf16[3,4,64,128]{3,2,0,1:T(8,128)(2,1)}), bf16[3,4,64,128]{3,2,0,1:T(8,128)(2,1)S(1)}, u32[]{:S(2)}, u32[]{:S(2)}) async-start(bf16[3,4,64,128]{3,2,0,1:T(8,128)(2,1)} %bitcast.33), calls=%async_computation.1 | async-start | bytes 393216 | tf_op jit(solution)/shard_map/all_to_all | solution.py:77
  80.2 8.2 %all-to-all-done.1 = bf16[3,4,64,128]{3,2,0,1:T(8,128)(2,1)S(1)} async-done(((bf16[3,4,64,128]{3,2,0,1:T(8,128)(2,1)}), bf16[3,4,64,128]{3,2,0,1:T(8,128)(2,1)S(1)}, u32[]{:S(2)}, u32[]{:S(2)}) %all-to-all-start.1) | async-done | bytes 196640 | tf_op jit(solution)/shard_map/all_to_all | solution.py:77
  88.5 0.2 copy.25
  88.6 0.7 gather_fusion.1
  89.4 4.4 %convolution_bitcast_fusion = f32[3,128,128]{2,0,1:T(4,128)S(1)} fusion(bf16[128,128,128]{2,1,0:T(8,128)(2,1)} %param.13, bf16[128,3,128]{2,1,0:T(4,128)(2,1)S(1)} %gather_fusion.1), kind=kOutput, calls=%fused_computation.22 | convolution fusion | flops 12582912 | bytes 4489216 | tf_op jit(solution)/shard_map/kij,ckj->cki/dot_general | solution.py:79
  93.9 0.7 reshape.104
  (19 shorter events, 0.5 us)
Async XLA Ops:
  4.2 40.8 %copy-start.1 = (u32[32]{0:T(128)S(1)}, u32[32]{0:T(128)}, u32[]{:S(2)}) copy-start(u32[32]{0:T(128)} %constant.69) | copy-start | bytes 388
  4.8 70.2 %all-to-all-start = ((s32[4,1,64]{2,1,0:T(1,128)}), s32[4,1,64]{2,1,0:T(1,128)S(1)}, u32[]{:S(2)}, u32[]{:S(2)}) async-start(s32[4,1,64]{2,1,0:T(1,128)} %all_to_all.9), calls=%async_computation | async-start | bytes 4096 | tf_op jit(solution)/shard_map/all_to_all | solution.py:71
  74.8 19.8 %copy-start = (bf16[3,4,4096]{2,1,0:T(4,128)(2,1)}, bf16[3,4,4096]{2,1,0:T(4,128)(2,1)S(1)}, u32[]{:S(2)}) copy-start(bf16[3,4,4096]{2,1,0:T(4,128)(2,1)S(1)} %fusion.4) | copy-start | bytes 294916
  76.9 11.6 %all-to-all-start.1 = ((bf16[3,4,64,128]{3,2,0,1:T(8,128)(2,1)}), bf16[3,4,64,128]{3,2,0,1:T(8,128)(2,1)S(1)}, u32[]{:S(2)}, u32[]{:S(2)}) async-start(bf16[3,4,64,128]{3,2,0,1:T(8,128)(2,1)} %bitcast.33), calls=%async_computation.1 | async-start | bytes 393216 | tf_op jit(solution)/shard_map/all_to_all | solution.py:77
where the time goes:
time: 95 us; the launch traced here: 94.6 us
  blocking collectives  31.1 us (33%)
  other arithmetic  19.8 us (21%)
  matrix products  14.4 us (15%)
  starting transfers between devices  9.71 us (10%)
  local copies, waits for them, and re-layouts  9.33 us (10%)
  waiting for transfers between devices  8.21 us (9%)
  between operations  2.1 us (2%)
    unnamed x2, blocking collectives  24.3 us
    cos x1, other arithmetic, synthesize(): right = jnp.concatenate([jnp.cos(angle), jnp.sin(angle)], axis=0)  16.6 us
    all_to_all x1, waiting for transfers between devices, local(): lax.all_to_all(picked, 'band', split_axis=1, concat_axis=1, tiled=True)  8.21 us
    all_gather x1, blocking collectives, local(): lax.all_gather(coeffs, 'ord', axis=2, tiled=True)  6.72 us
    all_to_all x1, starting transfers between devices, local(): lax.all_to_all(requests, 'band', split_axis=0, concat_axis=0, tiled=True)  6.35 us
    dot_general x1, matrix products, local(): jnp.einsum('rml,cml->rcm', legendre, alm, preferred_element_type=jnp.floa...  5.76 us
    dot_general x1, matrix products, local(): jnp.einsum('kij,ckj->cki', weights, source, preferred_element_type=jnp.fl...  4.43 us
    dot_general x1, matrix products, synthesize(): jnp.dot(left, right, precision=lax.Precision.HIGHEST, preferred_element_t...  4.16 us
  transfers between devices with their start and end apart: 2, of which 1 were waited for; matrix products, arithmetic and copies ran while one was open for 33% of the time, Pallas kernels for 0%

commit v1 on v0

v1 whole, which is shorter than its diff:
```python
import functools
import math

import jax
import jax.numpy as jnp
from jax import lax
from jax.experimental import pallas as pl
from jax.experimental.pallas import tpu as pltpu
from jax.sharding import PartitionSpec as P

LANES = 128
GROUP = 16
NT = (((1,), (1,)), ((), ()))
SINE = (6.2831851600887045, -41.34165503125142, 81.60100406374923, -76.54978209038376, 39.53670461908883)


def sin_turns(v):
    z = v * v
    total = SINE[-1]
    for term in SINE[-2::-1]:
        total = total * z + term
    return total * v


def wrap(u):
    return u - jnp.round(u)


def cos_turns(u):
    return sin_turns(0.25 - jnp.abs(u))


def split(x):
    high = x.astype(jnp.bfloat16)
    return high, (x - high.astype(jnp.float32)).astype(jnp.bfloat16)


def analysis(band_ref, cycle_ref, orders_ref, legendre_hbm, alm_hbm, out_ref, legendre, alm, sems):
    cycles, orders, _ = legendre.shape
    parts = alm.shape[0]
    half = parts // 2
    groups = orders // GROUP
    copies = []
    for g in range(groups):
        rows = pl.ds(g * GROUP, GROUP)
        pair = (
            pltpu.make_async_copy(alm_hbm.at[:, rows], alm.at[:, rows], sems.at[0, g]),
            pltpu.make_async_copy(legendre_hbm.at[:, rows], legendre.at[:, rows], sems.at[1, g]),
        )
        for copy in pair:
            copy.start()
        copies.append(pair)

    band = band_ref[0]
    cycles_here = cycle_ref.shape[0]
    row = lax.broadcasted_iota(jnp.int32, (cycles, LANES // 2), 0)
    parity = jnp.zeros((cycles, LANES // 2), jnp.float32)
    for i in range(cycles_here):
        odd = (cycle_ref[i] % 2).astype(jnp.float32)
        parity = jnp.where(row == band * cycles_here + i, odd, parity)
    ids = orders_ref[...].astype(jnp.float32) * jnp.where(band == 0, 1.0, 0.0)
    base = half * 2 * orders
    out_ref[:, base : base + orders] = jnp.broadcast_to(ids, (cycles, orders))
    out_ref[:, base + orders : base + 2 * orders] = parity

    width = parts * GROUP
    rows_of = lax.broadcasted_iota(jnp.int32, (cycles * GROUP, width), 0) % GROUP
    lane_of = lax.broadcasted_iota(jnp.int32, (cycles * GROUP, width), 1) % GROUP
    same = rows_of == lane_of
    sums = []
    for g in range(groups):
        for copy in copies[g]:
            copy.wait()
        rows = slice(g * GROUP, (g + 1) * GROUP)
        left = legendre[:, rows, :].reshape(cycles * GROUP, -1)
        right = alm[:, rows, :].reshape(width, -1)
        full = lax.dot_general(left, right, NT, preferred_element_type=jnp.float32)
        full = jnp.where(same, full, 0.0)
        sums.append(jnp.sum(full.reshape(cycles, GROUP, width), axis=1))
    for f in range(half):
        pieces = [sums[g][:, c * GROUP : (c + 1) * GROUP] for c in (f, f + half) for g in range(groups)]
        out_ref[:, 2 * f * orders : 2 * (f + 1) * orders] = jnp.concatenate(pieces, axis=1)


def lens(n_ord, cycles_here, fields, place_ref, src_band_ref, src_block_ref, *refs):
    arrays = refs[:n_ord]
    weights_hbm, sky_out, lensed_out, sky, stage, weights, sem = refs[n_ord:]
    load = pltpu.make_async_copy(weights_hbm, weights, sem)
    load.start()

    band, slot = place_ref[0], place_ref[1].astype(jnp.float32)
    cycles = arrays[0].shape[0]
    half = LANES // 2
    npix_here = sky_out.shape[2]
    npix = npix_here * n_ord
    cols = npix_here // LANES
    q_len = min(512, npix_here)
    p_len = npix_here // q_len
    rows_col = fields * cycles

    lane = lax.broadcasted_iota(jnp.int32, (cycles, LANES), 1)
    low = lane < half
    low_row = low[0:1]
    meta = [a[:, fields * LANES :] for a in arrays]
    ids = [jnp.where(low_row, m[0:1], pltpu.roll(m, half, 1)[0:1]) for m in meta]
    odd = jnp.where(low, pltpu.roll(meta[0], half, 1), meta[0]) > 0.5

    q_iota = lax.broadcasted_iota(jnp.int32, (LANES, q_len), 1).astype(jnp.float32) * (1.0 / npix)
    shift = jnp.where(lax.broadcasted_iota(jnp.int32, (LANES, q_len), 0) < half, 0.0, 0.25)
    table_high, table_low = [], []
    for a in range(n_ord):
        column = jnp.broadcast_to(ids[a], (LANES, LANES)).T
        column = jnp.concatenate([column] * (q_len // LANES), axis=1)
        high, low_part = split(cos_turns(wrap(column * q_iota - shift)))
        table_high.append(high)
        table_low.append(low_part)
    table_high = jnp.concatenate(table_high, axis=0)
    table_low = jnp.concatenate(table_low, axis=0)

    p_iota = lax.broadcasted_iota(jnp.int32, (p_len, LANES), 0).astype(jnp.float32) * (q_len / npix)
    low_p = lax.broadcasted_iota(jnp.int32, (p_len, LANES), 1) < half
    left_rows = [[None] * n_ord for _ in range(p_len)]
    for a in range(n_ord):
        m = ids[a]
        factor = jnp.where(m == 0.0, 1.0, 2.0)
        start = wrap(m * (slot * (1.0 / n_ord)))
        even_turn = wrap(wrap(m * p_iota) + start)
        odd_turn = wrap(even_turn + wrap(m * (0.5 / npix)))
        terms = []
        for turn in (even_turn, odd_turn):
            cosine = cos_turns(turn) * factor
            sine = cos_turns(wrap(turn - 0.25)) * factor
            terms.append((jnp.where(low_p, cosine, -cosine), -sine))
        x = [arrays[a][:, f * LANES : (f + 1) * LANES] for f in range(fields)]
        turned = [pltpu.roll(v, half, 1) for v in x]
        for p in range(p_len):
            straight = jnp.where(odd, terms[1][0][p : p + 1], terms[0][0][p : p + 1])
            crossed = jnp.where(odd, terms[1][1][p : p + 1], terms[0][1][p : p + 1])
            left_rows[p][a] = jnp.concatenate(
                [x[f] * straight + turned[f] * crossed for f in range(fields)], axis=0
            )
    for p in range(p_len):
        high, low_part = split(jnp.concatenate(left_rows[p], axis=1))
        dot = functools.partial(jnp.dot, preferred_element_type=jnp.float32)
        pixels = dot(high, table_high) + (dot(low_part, table_high) + dot(high, table_low))
        pixels = pixels.astype(jnp.bfloat16).astype(jnp.float32)
        for j in range(q_len // LANES):
            col = p * (q_len // LANES) + j
            sky[col * rows_col : (col + 1) * rows_col, :] = pixels[:, j * LANES : (j + 1) * LANES]

    first = pl.multiple_of(band * cycles_here, cycles_here)
    for col in range(cols):
        for f in range(fields):
            own = sky[pl.ds(col * rows_col + f * cycles + first, cycles_here), :]
            sky_out[f, :, col * LANES : (col + 1) * LANES] = own.astype(jnp.bfloat16)

    stage[...] = jnp.zeros_like(stage)
    for col in range(cols):
        for c in range(cycles_here):
            k = c * cols + col
            block = src_block_ref[k]
            cycle = src_band_ref[k] * cycles_here + block // cols
            begin = (block % cols) * rows_col + cycle
            source = sky[pl.ds(begin, fields, stride=cycles), :]
            stage[2 * col + c % 2, pl.ds(c, fields, stride=cycles_here), :] = source

    load.wait()
    rows = stage.shape[1]
    cycle_of = lax.broadcasted_iota(jnp.int32, (rows, LANES), 0) % cycles_here
    for col in range(cols):
        left = jnp.concatenate([stage[2 * col], stage[2 * col + 1]], axis=1).astype(jnp.bfloat16)
        right = jnp.concatenate(
            [
                jnp.concatenate([weights[c * cols + col], weights[(c + 1) * cols + col]], axis=1)
                for c in range(0, cycles_here, 2)
            ],
            axis=0,
        )
        full = lax.dot_general(left, right, NT, preferred_element_type=jnp.float32)
        out = full[:, 0:LANES]
        for n in range(1, cycles_here // 2):
            out = jnp.where(cycle_of // 2 == n, full[:, n * LANES : (n + 1) * LANES], out)
        for f in range(fields):
            lensed_out[f, :, col * LANES : (col + 1) * LANES] = out[f * cycles_here : (f + 1) * cycles_here]


def turned(x, axis, n):
    return [lax.ppermute(x, axis, [(i, (i + k) % n) for i in range(n)]) for k in range(1, n)]


def local(alm, legendre, order_ids, cycle_number, src_band, src_block, weights):
    n_band, n_ord = lax.axis_size("band"), lax.axis_size("ord")
    parts, orders, _ = alm.shape
    fields = parts // 2
    cycles = legendre.shape[0]
    cycles_here = cycle_number.shape[0]
    blocks, blk, _ = weights.shape
    npix_here = blocks * blk // cycles_here
    band, slot = lax.axis_index("band"), lax.axis_index("ord")
    place = jnp.stack([band, slot]).astype(jnp.int32)
    width = (fields + 1) * 2 * orders
    smem = pl.BlockSpec(memory_space=pltpu.SMEM)
    vmem = pl.BlockSpec(memory_space=pltpu.VMEM)
    anywhere = pl.BlockSpec(memory_space=pl.ANY)
    part = pl.pallas_call(
        analysis,
        name="analysis",
        out_shape=jax.ShapeDtypeStruct((cycles, width), jnp.float32),
        in_specs=[smem, smem, vmem, anywhere, anywhere],
        out_specs=vmem,
        scratch_shapes=[
            pltpu.VMEM(legendre.shape, legendre.dtype),
            pltpu.VMEM(alm.shape, alm.dtype),
            pltpu.SemaphoreType.DMA((2, orders // GROUP)),
        ],
    )(place, cycle_number, order_ids[None], legendre, alm)
    if n_band <= 8:
        total = sum(turned(part, "band", n_band), part)
    else:
        total = lax.psum(part, "band")
    arrays = [total] + turned(total, "ord", n_ord)
    cols = npix_here // blk
    sky_map, lensed = pl.pallas_call(
        functools.partial(lens, n_ord, cycles_here, fields),
        name="lens",
        out_shape=(
            jax.ShapeDtypeStruct((fields, cycles_here, npix_here), jnp.bfloat16),
            jax.ShapeDtypeStruct((fields, cycles_here, npix_here), jnp.float32),
        ),
        in_specs=[smem, smem, smem] + [vmem] * n_ord + [anywhere],
        out_specs=(vmem, vmem),
        scratch_shapes=[
            pltpu.VMEM((cols * fields * cycles, blk), jnp.float32),
            pltpu.VMEM((2 * cols, 16, blk), jnp.float32),
            pltpu.VMEM(weights.shape, weights.dtype),
            pltpu.SemaphoreType.DMA,
        ],
    )(place, src_band[:, 0], src_block, *arrays, weights)
    return sky_map, lensed


def solution(mesh):
    placed = (
        P("sim", "ord", "band"),
        P(None, "ord", "band"),
        P("ord"),
        P("band"),
        P(("sim", "band", "ord"), None),
        P(("sim", "band", "ord")),
        P(("sim", "band", "ord"), None, None),
    )
    return jax.shard_map(
        local,
        mesh=mesh,
        in_specs=placed,
        out_specs=(P("sim", "band", "ord"), P("sim", "band", "ord")),
        check_vma=False,
    )
```

time: 95 us -> 33.3 us (0.35)
  blocking collectives: 31.1 us -> 0 us
  other arithmetic: 19.8 us -> 1.33 us
  matrix products: 14.4 us -> 0 us
  Pallas kernels: 0 us -> 14.4 us
  local copies, waits for them, and re-layouts: 9.33 us -> 0.6 us
  starting transfers between devices: 9.71 us -> 7.91 us
  between operations: 2.1 us -> 0.67 us
    unnamed x2 -> x0, blocking collectives: 24.3 us -> none
    cos x2 -> x0, other arithmetic: 16.7 us -> none  [the longest x1 16.6 us: synthesize(): right = jnp.concatenate([jnp.cos(angle), jnp.sin(angle)], axis=0)]
    pallas_call x0 -> x2, Pallas kernels: none -> 14.4 us  [the longest x1 8.83 us: local(): pl.pallas_call(functools.partial(lens, n_ord, cycles_here, fields), name=...]
    dot_general x3 -> x0, matrix products: 14.4 us -> none  [the longest x1 5.76 us: local(): jnp.einsum('rml,cml->rcm', legendre, alm, preferred_element_type=jnp.floa...]
    all_to_all x2 -> x0, starting transfers between devices: 9.71 us -> none  [the longest x1 6.35 us: local(): lax.all_to_all(requests, 'band', split_axis=0, concat_axis=0, tiled=True)]
    all_to_all x2 -> x0, waiting for transfers between devices: 8.21 us -> none  [the longest x1 8.21 us: local(): lax.all_to_all(picked, 'band', split_axis=1, concat_axis=1, tiled=True)]
    ppermute x0 -> x6, waiting for transfers between devices: none -> 8.09 us  [turned(): lax.ppermute(x, axis, [(i, (i + k) % n) for i in range(n)])]
    ppermute x0 -> x6, starting transfers between devices: none -> 7.91 us  [turned(): lax.ppermute(x, axis, [(i, (i + k) % n) for i in range(n)])]
  transfers between devices with their start and end apart: 2 -> 6, of which waited for: 1 -> 5; matrix products, arithmetic and copies ran while one was open for 33% -> 0% of each run, Pallas kernels for 0% -> 0%
where the time goes in v1:
time: 33.3 us; the launch traced here: 33 us
  Pallas kernels  14.4 us (43%)
  waiting for transfers between devices  8.09 us (24%)
  starting transfers between devices  7.91 us (24%)
  other arithmetic  1.33 us (4%)
  between operations  0.67 us (2%)
  local copies, waits for them, and re-layouts  0.6 us (2%)
    pallas_call x1, Pallas kernels, local(): pl.pallas_call(functools.partial(lens, n_ord, cycles_here, fields), name=...  8.83 us
    ppermute x6, waiting for transfers between devices, turned(): lax.ppermute(x, axis, [(i, (i + k) % n) for i in range(n)])  8.09 us
    ppermute x6, starting transfers between devices, turned(): lax.ppermute(x, axis, [(i, (i + k) % n) for i in range(n)])  7.91 us
    pallas_call x1, Pallas kernels, local(): pl.pallas_call(analysis, name='analysis', out_shape=jax.ShapeDtypeStruct(...  5.54 us
    add x1, other arithmetic, local(): total = sum(turned(part, 'band', n_band), part)  0.77 us
  transfers between devices with their start and end apart: 6, of which 5 were waited for; matrix products, arithmetic and copies ran while one was open for 0% of the time, Pallas kernels for 0%

profile of v1, /device:TPU:0, one launch (start us, length us, event | category | flops | bytes accessed | tf_op | source)
XLA Modules:
  0.0 33.0 jit_solution(14655527555329548960)
XLA Ops:
  0.6 0.6 %pad_add_fusion.band_ref.place_ref = s32[2]{0:T(128)} fusion(s32[1]{0:T(128)} %bitcast.1, s32[1]{0:T(128)} %bitcast), kind=kLoop, calls=%fused_computation.1 | loop fusion | flops 2 | bytes 16 | tf_op jit(solution)/shard_map/stack | solution.py:200
  1.2 5.5 %analysis.1 = f32[16,512]{1,0:T(8,128)} custom-call(s32[2]{0:T(128)} %pad_add_fusion.band_ref.place_ref, s32[4]{0:T(128)} %cycle_ref.1, s32[1,64]{1,0:T(1,128)} %bitcast.4, bf16[16,64,2048]{2,1,0:T(8,128)(2,1)} %legendre_hbm.1, bf16[6,64,2048]{2,1,0:T(8,128)(2,1)} %alm_hbm.1), custom_call_target="tpu_custom_call" | custom-call | tf_op jit(solution)/shard_map/analysis/pallas_call | solution.py:205
  6.7 5.1 %collective-permute-start.2 = (f32[16,512]{1,0:T(8,128)}, f32[16,512]{1,0:T(8,128)S(1)}, u32[]{:S(2)}, u32[]{:S(2)}) collective-permute-start(f32[16,512]{1,0:T(8,128)} %analysis.1), channel_id=1, source_target_pairs={{0,12},{4,0},{8,4},{12,8},{1,13},{5,1},{9,5},{13,9},{2,14},{6,2},{... | collective-permute-start | bytes 98312 | tf_op jit(solution)/shard_map/ppermute | solution.py:188
  11.9 0.0 collective-permute-start.1
  11.9 1.0 %collective-permute-start = (f32[16,512]{1,0:T(8,128)}, f32[16,512]{1,0:T(8,128)S(1)}, u32[]{:S(2)}, u32[]{:S(2)}) collective-permute-start(f32[16,512]{1,0:T(8,128)} %analysis.1), channel_id=1, source_target_pairs={{0,4},{4,8},{8,12},{12,0},{1,5},{5,9},{9,13},{13,1},{2,6},{6,10},{... | collective-permute-start | bytes 98312 | tf_op jit(solution)/shard_map/ppermute | solution.py:188
  12.9 0.9 %collective-permute-done.2 = f32[16,512]{1,0:T(8,128)S(1)} collective-permute-done((f32[16,512]{1,0:T(8,128)}, f32[16,512]{1,0:T(8,128)S(1)}, u32[]{:S(2)}, u32[]{:S(2)}) %collective-permute-start.2) | collective-permute-done | bytes 32800 | tf_op jit(solution)/shard_map/ppermute | solution.py:188
  13.8 3.1 %collective-permute-done.1 = f32[16,512]{1,0:T(8,128)S(1)} collective-permute-done((f32[16,512]{1,0:T(8,128)}, f32[16,512]{1,0:T(8,128)S(1)}, u32[]{:S(2)}, u32[]{:S(2)}) %collective-permute-start.1) | collective-permute-done | bytes 32800 | tf_op jit(solution)/shard_map/ppermute | solution.py:188
  16.9 0.9 %collective-permute-done = f32[16,512]{1,0:T(8,128)S(1)} collective-permute-done((f32[16,512]{1,0:T(8,128)}, f32[16,512]{1,0:T(8,128)S(1)}, u32[]{:S(2)}, u32[]{:S(2)}) %collective-permute-start) | collective-permute-done | bytes 32800 | tf_op jit(solution)/shard_map/ppermute | solution.py:188
  17.8 0.8 %add_add_fusion.refs_0_ = f32[16,512]{1,0:T(8,128)S(1)} fusion(f32[16,512]{1,0:T(8,128)S(1)} %collective-permute-done.2, f32[16,512]{1,0:T(8,128)S(1)} %collective-permute-done.1, f32[16,512]{1,0:T(8,128)} %analysis.1, f32[16,512]{1,0:T(8,128)S(1)} %collective-permute-done), kind=kLoop, calls=%fused_computation | loop fusion | flops 24576 | bytes 163840 | tf_op jit(solution)/shard_map/add | solution.py:218
  18.6 0.0 copy-start
  18.6 0.1 collective-permute-start.5
  18.6 1.6 %collective-permute-start.4 = (f32[16,512]{1,0:T(8,128)S(1)}, f32[16,512]{1,0:T(8,128)S(1)}, u32[]{:S(2)}, u32[]{:S(2)}) collective-permute-start(f32[16,512]{1,0:T(8,128)S(1)} %add_add_fusion.refs_0_), channel_id=1, source_target_pairs={{0,2},{1,3},{2,0},{3,1},{4,6},{5,7},{6,4},{7,5},{8,10},{9,11},{10,... | collective-permute-start | bytes 98312 | tf_op jit(solution)/shard_map/ppermute | solution.py:188
  20.2 0.2 collective-permute-start.3
  20.4 0.0 collective-permute-done.5.refs_3_
  20.4 0.0 copy-start.1
  20.4 2.4 %collective-permute-done.4.refs_2_ = f32[16,512]{1,0:T(8,128)S(1)} collective-permute-done((f32[16,512]{1,0:T(8,128)S(1)}, f32[16,512]{1,0:T(8,128)S(1)}, u32[]{:S(2)}, u32[]{:S(2)}) %collective-permute-start.4) | collective-permute-done | bytes 32800 | tf_op jit(solution)/shard_map/ppermute | solution.py:188
  22.7 0.0 copy-start.2
  22.7 0.8 %collective-permute-done.3.refs_1_ = f32[16,512]{1,0:T(8,128)S(1)} collective-permute-done((f32[16,512]{1,0:T(8,128)S(1)}, f32[16,512]{1,0:T(8,128)S(1)}, u32[]{:S(2)}, u32[]{:S(2)}) %collective-permute-start.3) | collective-permute-done | bytes 32800 | tf_op jit(solution)/shard_map/ppermute | solution.py:188
  23.5 0.0 copy-start.3
  23.5 0.0 copy-done
  23.5 0.0 copy-done.1
  23.5 0.0 copy-done.2
  23.6 0.6 %copy-done.3 = f32[16,512]{1,0:T(8,128)} copy-done((f32[16,512]{1,0:T(8,128)}, f32[16,512]{1,0:T(8,128)S(1)}, u32[]{:S(2)}) %copy-start.3) | copy-done | bytes 32792
  24.1 8.8 %lens.1 = (bf16[3,4,4096]{2,1,0:T(4,128)(2,1)}, f32[3,4,4096]{2,1,0:T(4,128)}) custom-call(s32[2]{0:T(128)} %pad_add_fusion.band_ref.place_ref, s32[128]{0:T(128)} %bitcast.5, s32[128]{0:T(128)} %src_block_ref.1, f32[16,512]{1,0:T(8,128)} %copy-done, f32[16,512]{1,0:T(8,128)} %copy-done.3, f32[16,512]{1,0:T(8,128)} %copy-done.2, f32[16,512]{1,0:T(8,128)} %copy-done.1, ...), custom_call_target="tpu_custom_call" | custom-call | tf_op jit(solution)/shard_map/lens/pallas_call | solution.py:223
Async XLA Ops:
  6.7 7.0 %collective-permute-start.2 = (f32[16,512]{1,0:T(8,128)}, f32[16,512]{1,0:T(8,128)S(1)}, u32[]{:S(2)}, u32[]{:S(2)}) collective-permute-start(f32[16,512]{1,0:T(8,128)} %analysis.1), channel_id=1, source_target_pairs={{0,12},{4,0},{8,4},{12,8},{1,13},{5,1},{9,5},{13,9},{2,14},{6,2},{... | collective-permute-start | bytes 98312 | tf_op jit(solution)/shard_map/ppermute | solution.py:188
  11.9 5.0 %collective-permute-start.1 = (f32[16,512]{1,0:T(8,128)}, f32[16,512]{1,0:T(8,128)S(1)}, u32[]{:S(2)}, u32[]{:S(2)}) collective-permute-start(f32[16,512]{1,0:T(8,128)} %analysis.1), channel_id=1, source_target_pairs={{0,8},{4,12},{8,0},{12,4},{1,9},{5,13},{9,1},{13,5},{2,10},{6,14},... | collective-permute-start | bytes 98312 | tf_op jit(solution)/shard_map/ppermute | solution.py:188
  11.9 5.9 %collective-permute-start = (f32[16,512]{1,0:T(8,128)}, f32[16,512]{1,0:T(8,128)S(1)}, u32[]{:S(2)}, u32[]{:S(2)}) collective-permute-start(f32[16,512]{1,0:T(8,128)} %analysis.1), channel_id=1, source_target_pairs={{0,4},{4,8},{8,12},{12,0},{1,5},{5,9},{9,13},{13,1},{2,6},{6,10},{... | collective-permute-start | bytes 98312 | tf_op jit(solution)/shard_map/ppermute | solution.py:188
  18.6 5.0 %copy-start = (f32[16,512]{1,0:T(8,128)}, f32[16,512]{1,0:T(8,128)S(1)}, u32[]{:S(2)}) copy-start(f32[16,512]{1,0:T(8,128)S(1)} %add_add_fusion.refs_0_) | copy-start | bytes 98308
  18.6 1.8 %collective-permute-start.5 = (f32[16,512]{1,0:T(8,128)S(1)}, f32[16,512]{1,0:T(8,128)S(1)}, u32[]{:S(2)}, u32[]{:S(2)}) collective-permute-start(f32[16,512]{1,0:T(8,128)S(1)} %add_add_fusion.refs_0_), channel_id=1, source_target_pairs={{0,3},{1,0},{2,1},{3,2},{4,7},{5,4},{6,5},{7,6},{8,11},{9,8},{10,9... | collective-permute-start | bytes 98312 | tf_op jit(solution)/shard_map/ppermute | solution.py:188
  18.6 4.1 %collective-permute-start.4 = (f32[16,512]{1,0:T(8,128)S(1)}, f32[16,512]{1,0:T(8,128)S(1)}, u32[]{:S(2)}, u32[]{:S(2)}) collective-permute-start(f32[16,512]{1,0:T(8,128)S(1)} %add_add_fusion.refs_0_), channel_id=1, source_target_pairs={{0,2},{1,3},{2,0},{3,1},{4,6},{5,7},{6,4},{7,5},{8,10},{9,11},{10,... | collective-permute-start | bytes 98312 | tf_op jit(solution)/shard_map/ppermute | solution.py:188
  20.2 3.3 %collective-permute-start.3 = (f32[16,512]{1,0:T(8,128)S(1)}, f32[16,512]{1,0:T(8,128)S(1)}, u32[]{:S(2)}, u32[]{:S(2)}) collective-permute-start(f32[16,512]{1,0:T(8,128)S(1)} %add_add_fusion.refs_0_), channel_id=1, source_target_pairs={{0,1},{1,2},{2,3},{3,0},{4,5},{5,6},{6,7},{7,4},{8,9},{9,10},{10,1... | collective-permute-start | bytes 98312 | tf_op jit(solution)/shard_map/ppermute | solution.py:188
  20.4 3.2 %copy-start.1 = (f32[16,512]{1,0:T(8,128)}, f32[16,512]{1,0:T(8,128)S(1)}, u32[]{:S(2)}) copy-start(f32[16,512]{1,0:T(8,128)S(1)} %collective-permute-done.5.refs_3_) | copy-start | bytes 98308
  22.7 0.8 %copy-start.2 = (f32[16,512]{1,0:T(8,128)}, f32[16,512]{1,0:T(8,128)S(1)}, u32[]{:S(2)}) copy-start(f32[16,512]{1,0:T(8,128)S(1)} %collective-permute-done.4.refs_2_) | copy-start | bytes 98308
  23.5 0.6 %copy-start.3 = (f32[16,512]{1,0:T(8,128)}, f32[16,512]{1,0:T(8,128)S(1)}, u32[]{:S(2)}) copy-start(f32[16,512]{1,0:T(8,128)S(1)} %collective-permute-done.3.refs_1_) | copy-start | bytes 98308

commit v2 on v1

v2 whole, which is shorter than its diff:
```python
import functools
import math

import jax
import jax.numpy as jnp
from jax import lax
from jax.experimental import pallas as pl
from jax.experimental.pallas import tpu as pltpu
from jax.sharding import PartitionSpec as P

LANES = 128
GROUP = 16
Q_LEN = 512
CHUNKS = 4
NT = (((1,), (1,)), ((), ()))
SINE = (6.2831851600887045, -41.34165503125142, 81.60100406374923, -76.54978209038376, 39.53670461908883)


def sin_turns(v):
    z = v * v
    total = SINE[-1]
    for term in SINE[-2::-1]:
        total = total * z + term
    return total * v


def wrap(u):
    return u - jnp.round(u)


def cos_turns(u):
    return sin_turns(0.25 - jnp.abs(u))


def split(x):
    high = x.astype(jnp.bfloat16)
    return high, (x - high.astype(jnp.float32)).astype(jnp.bfloat16)


def analysis(cycle_hbm, orders_hbm, legendre_hbm, alm_hbm, out_ref, legendre, alm, cycle_ref, orders_ref, sems):
    cycles, orders, _ = legendre.shape
    parts = alm.shape[0]
    half = parts // 2
    groups = orders // GROUP
    copies = []
    for g in range(groups):
        rows = pl.ds(g * GROUP, GROUP)
        copies.append(
            (
                pltpu.make_async_copy(alm_hbm.at[:, rows], alm.at[:, rows], sems.at[2 * g]),
                pltpu.make_async_copy(legendre_hbm.at[:, rows], legendre.at[:, rows], sems.at[2 * g + 1]),
            )
        )
    small = (
        pltpu.make_async_copy(cycle_hbm, cycle_ref, sems.at[2 * groups]),
        pltpu.make_async_copy(orders_hbm, orders_ref, sems.at[2 * groups + 1]),
    )
    for pair in copies[:1] + [small] + copies[1:]:
        for copy in pair:
            copy.start()

    for copy in small:
        copy.wait()
    band = lax.axis_index("band")
    cycles_here = cycle_ref.shape[0]
    row = lax.broadcasted_iota(jnp.int32, (cycles, LANES // 2), 0)
    parity = jnp.zeros((cycles, LANES // 2), jnp.float32)
    for i in range(cycles_here):
        odd = (cycle_ref[i] & 1).astype(jnp.float32)
        parity = jnp.where(row == band * cycles_here + i, odd, parity)
    ids = orders_ref[...].astype(jnp.float32) * jnp.where(band == 0, 1.0, 0.0)
    base = half * 2 * orders
    out_ref[:, base : base + orders] = jnp.broadcast_to(ids, (cycles, orders))
    out_ref[:, base + orders : base + 2 * orders] = parity

    width = parts * GROUP
    share = cycles // 2
    rows_of = lax.broadcasted_iota(jnp.int32, (share * GROUP, width), 0) % GROUP
    lane_of = lax.broadcasted_iota(jnp.int32, (share * GROUP, width), 1) % GROUP
    same = rows_of == lane_of
    sums = []
    for g in range(groups):
        for copy in copies[g]:
            copy.wait()
        rows = slice(g * GROUP, (g + 1) * GROUP)
        right = alm[:, rows, :].reshape(width, -1)
        both = []
        for h in range(2):
            left = legendre[h * share : (h + 1) * share, rows, :].reshape(share * GROUP, -1)
            full = lax.dot_general(left, right, NT, preferred_element_type=jnp.float32)
            full = jnp.where(same, full, 0.0)
            both.append(jnp.sum(full.reshape(share, GROUP, width), axis=1))
        sums.append(jnp.concatenate(both, axis=0))
    for f in range(half):
        pieces = [sums[g][:, c * GROUP : (c + 1) * GROUP] for c in (f, f + half) for g in range(groups)]
        out_ref[:, 2 * f * orders : 2 * (f + 1) * orders] = jnp.concatenate(pieces, axis=1)


def fetch(part_ref, weights_hbm, part_out, weights_ref, sem):
    copy = pltpu.make_async_copy(weights_hbm, weights_ref, sem)
    copy.start()
    part_out[...] = part_ref[...]
    copy.wait()


def synthesis(n_ord, fields, npix_here, arrays):
    slot = lax.axis_index("ord").astype(jnp.float32)
    cycles = arrays[0].shape[0]
    half = LANES // 2
    npix = npix_here * n_ord
    q_len = min(Q_LEN, npix_here)
    p_len = npix_here // q_len

    lane = lax.broadcasted_iota(jnp.int32, (cycles, LANES), 1)
    low = lane < half
    low_row = low[0:1]
    meta = [a[:, fields * LANES :] for a in arrays]
    ids = [jnp.where(low_row, m[0:1], pltpu.roll(m, half, 1)[0:1]) for m in meta]
    odd = jnp.where(low, pltpu.roll(meta[0], half, 1), meta[0]) > 0.5

    q_iota = lax.broadcasted_iota(jnp.int32, (LANES, q_len), 1).astype(jnp.float32) * (1.0 / npix)
    shift = jnp.where(lax.broadcasted_iota(jnp.int32, (LANES, q_len), 0) < half, 0.0, 0.25)
    table = []
    for m in ids:
        column = jnp.broadcast_to(m, (LANES, LANES)).T
        column = jnp.concatenate([column] * (q_len // LANES), axis=1)
        table.append(split(cos_turns(wrap(column * q_iota - shift))))
    table_high, table_low = (jnp.concatenate(v, axis=0) for v in zip(*table))

    p_iota = lax.broadcasted_iota(jnp.int32, (p_len, LANES), 0).astype(jnp.float32) * (q_len / npix)
    low_p = lax.broadcasted_iota(jnp.int32, (p_len, LANES), 1) < half
    columns = []
    for a, m in zip(arrays, ids):
        factor = jnp.where(m == 0.0, 1.0, 2.0)
        start = wrap(m * (slot * (1.0 / n_ord)))
        even_turn = wrap(wrap(m * p_iota) + start)
        odd_turn = wrap(even_turn + wrap(m * (0.5 / npix)))
        terms = []
        for turn in (even_turn, odd_turn):
            cosine = cos_turns(turn) * factor
            sine = cos_turns(wrap(turn - 0.25)) * factor
            terms.append((jnp.where(low_p, cosine, -cosine), -sine))
        x = [a[:, f * LANES : (f + 1) * LANES] for f in range(fields)]
        crossed_x = [pltpu.roll(v, half, 1) for v in x]
        rows = []
        for p in range(p_len):
            straight = jnp.where(odd, terms[1][0][p : p + 1], terms[0][0][p : p + 1])
            crossed = jnp.where(odd, terms[1][1][p : p + 1], terms[0][1][p : p + 1])
            rows += [x[f] * straight + crossed_x[f] * crossed for f in range(fields)]
        columns.append(split(jnp.concatenate(rows, axis=0)))
    high, low_part = (jnp.concatenate(v, axis=1) for v in zip(*columns))
    dot = functools.partial(jnp.dot, preferred_element_type=jnp.float32)
    return dot(high, table_high) + (dot(low_part, table_high) + dot(high, table_low))


def near(n_ord, fields, npix_here, *refs):
    refs[-1][...] = synthesis(n_ord, fields, npix_here, [r[...] for r in refs[:-1]])


def lens(n_ord, cycles_here, fields, src_band_ref, src_block_ref, *refs):
    arrays = refs[: n_ord // 2]
    near_ref, weights, sky_hbm, lensed_hbm, sky, stage, sky_out, lensed_out, sems = refs[n_ord // 2 :]
    band = lax.axis_index("band")
    cycles = arrays[0].shape[0]
    npix_here = sky_out.shape[2]
    cols = npix_here // LANES
    q_len = near_ref.shape[1]
    p_len = npix_here // q_len
    rows_col = fields * cycles

    pixels = near_ref[...] + synthesis(n_ord, fields, npix_here, [r[...] for r in arrays])
    pixels = pixels.astype(jnp.bfloat16).astype(jnp.float32)
    for p in range(p_len):
        for j in range(q_len // LANES):
            col = p * (q_len // LANES) + j
            sky[col * rows_col : (col + 1) * rows_col, :] = pixels[
                p * rows_col : (p + 1) * rows_col, j * LANES : (j + 1) * LANES
            ]

    first = pl.multiple_of(band * cycles_here, cycles_here)
    for col in range(cols):
        for f in range(fields):
            own = sky[pl.ds(col * rows_col + f * cycles + first, cycles_here), :]
            sky_out[f, :, col * LANES : (col + 1) * LANES] = own.astype(jnp.bfloat16)
    copies = [pltpu.make_async_copy(sky_out, sky_hbm, sems.at[0])]
    copies[0].start()

    shift_bits = cols.bit_length() - 1
    stage[...] = jnp.zeros_like(stage)
    for col in range(cols):
        for c in range(cycles_here):
            k = c * cols + col
            block = src_block_ref[k]
            cycle = src_band_ref[k] * cycles_here + lax.shift_right_logical(block, shift_bits)
            begin = (block & (cols - 1)) * rows_col + cycle
            source = sky[pl.ds(begin, fields, stride=cycles), :]
            stage[2 * col + c % 2, pl.ds(c, fields, stride=cycles_here), :] = source

    rows = stage.shape[1]
    cycle_of = lax.broadcasted_iota(jnp.int32, (rows, LANES), 0) % cycles_here
    chunk = cols // CHUNKS
    for col in range(cols):
        left = jnp.concatenate([stage[2 * col], stage[2 * col + 1]], axis=1).astype(jnp.bfloat16)
        right = jnp.concatenate(
            [
                jnp.concatenate([weights[c * cols + col], weights[(c + 1) * cols + col]], axis=1)
                for c in range(0, cycles_here, 2)
            ],
            axis=0,
        )
        full = lax.dot_general(left, right, NT, preferred_element_type=jnp.float32)
        out = full[:, 0:LANES]
        for n in range(1, cycles_here // 2):
            out = jnp.where(cycle_of // 2 == n, full[:, n * LANES : (n + 1) * LANES], out)
        for f in range(fields):
            lensed_out[f, :, col * LANES : (col + 1) * LANES] = out[f * cycles_here : (f + 1) * cycles_here]
        if (col + 1) % chunk == 0:
            lanes = pl.ds((col + 1 - chunk) * LANES, chunk * LANES)
            copies.append(
                pltpu.make_async_copy(
                    lensed_out.at[:, :, lanes], lensed_hbm.at[:, :, lanes], sems.at[(col + 1) // chunk]
                )
            )
            copies[-1].start()
    for copy in copies:
        copy.wait()


def crossed(x, axis, n):
    return [lax.ppermute(x, axis, [(i, i ^ k) for i in range(n)]) for k in range(1, n)]


def local(alm, legendre, order_ids, cycle_number, src_band, src_block, weights):
    n_band, n_ord = lax.axis_size("band"), lax.axis_size("ord")
    parts, orders, _ = alm.shape
    fields = parts // 2
    cycles = legendre.shape[0]
    cycles_here = cycle_number.shape[0]
    blocks, blk, _ = weights.shape
    npix_here = blocks * blk // cycles_here
    width = (fields + 1) * 2 * orders
    cols = npix_here // blk
    q_len = min(Q_LEN, npix_here)
    smem = pl.BlockSpec(memory_space=pltpu.SMEM)
    vmem = pl.BlockSpec(memory_space=pltpu.VMEM)
    hbm = pl.BlockSpec(memory_space=pltpu.HBM)

    def far(*arrays):
        return [pltpu.with_memory_space_constraint(v, pltpu.HBM) for v in arrays]

    part = pl.pallas_call(
        analysis,
        name="analysis",
        out_shape=pltpu.VMEM((cycles, width), jnp.float32),
        in_specs=[hbm] * 4,
        out_specs=vmem,
        scratch_shapes=[
            pltpu.VMEM(legendre.shape, legendre.dtype),
            pltpu.VMEM(alm.shape, alm.dtype),
            pltpu.SMEM(cycle_number.shape, jnp.int32),
            pltpu.VMEM((1, orders), jnp.int32),
            pltpu.SemaphoreType.DMA((2 * (orders // GROUP) + 2,)),
        ],
        compiler_params=pltpu.CompilerParams(vmem_limit_bytes=16 << 20),
        cost_estimate=pl.CostEstimate(flops=2 << 30, bytes_accessed=6 << 20, transcendentals=0),
    )(*far(cycle_number, order_ids[None], legendre, alm))
    own, weights = pl.pallas_call(
        fetch,
        name="fetch",
        out_shape=(pltpu.VMEM(part.shape, part.dtype), pltpu.VMEM(weights.shape, weights.dtype)),
        in_specs=[vmem, hbm],
        out_specs=(vmem, vmem),
        scratch_shapes=[pltpu.SemaphoreType.DMA],
        compiler_params=pltpu.CompilerParams(vmem_limit_bytes=8 << 20),
        cost_estimate=pl.CostEstimate(flops=1 << 30, bytes_accessed=6 << 20, transcendentals=0),
    )(part, *far(weights))
    if n_band <= 8:
        total = sum(crossed(part, "band", n_band), own)
    else:
        total = lax.psum(own, "band")
    arrays = [total] + crossed(total, "ord", n_ord)
    first = pl.pallas_call(
        functools.partial(near, n_ord, fields, npix_here),
        name="near",
        out_shape=pltpu.VMEM((npix_here // q_len * fields * cycles, q_len), jnp.float32),
        in_specs=[vmem] * (n_ord // 2),
        out_specs=vmem,
        compiler_params=pltpu.CompilerParams(vmem_limit_bytes=16 << 20),
        cost_estimate=pl.CostEstimate(flops=1 << 30, bytes_accessed=1 << 20, transcendentals=0),
    )(*arrays[: n_ord // 2])
    pixels = (fields, cycles_here, npix_here)
    return pl.pallas_call(
        functools.partial(lens, n_ord, cycles_here, fields),
        name="lens",
        out_shape=(jax.ShapeDtypeStruct(pixels, jnp.bfloat16), jax.ShapeDtypeStruct(pixels, jnp.float32)),
        in_specs=[smem, smem] + [vmem] * (n_ord // 2 + 2),
        out_specs=(hbm, hbm),
        scratch_shapes=[
            pltpu.VMEM((cols * fields * cycles, blk), jnp.float32),
            pltpu.VMEM((2 * cols, 16, blk), jnp.float32),
            pltpu.VMEM(pixels, jnp.bfloat16),
            pltpu.VMEM(pixels, jnp.float32),
            pltpu.SemaphoreType.DMA((CHUNKS + 1,)),
        ],
        compiler_params=pltpu.CompilerParams(vmem_limit_bytes=32 << 20),
    )(src_band[:, 0], src_block, *arrays[n_ord // 2 :], first, weights)


def solution(mesh):
    placed = (
        P("sim", "ord", "band"),
        P(None, "ord", "band"),
        P("ord"),
        P("band"),
        P(("sim", "band", "ord"), None),
        P(("sim", "band", "ord")),
        P(("sim", "band", "ord"), None, None),
    )
    return jax.shard_map(
        local,
        mesh=mesh,
        in_specs=placed,
        out_specs=(P("sim", "band", "ord"), P("sim", "band", "ord")),
        check_vma=False,
    )
```

time: 33.3 us -> 23 us (0.69)
  Pallas kernels: 14.4 us -> 9.79 us
  waiting for transfers between devices: 8.09 us -> 4.36 us
  other arithmetic: 1.33 us -> 0.01 us
  local copies, waits for them, and re-layouts: 0.6 us -> 0.01 us
    pallas_call x1, Pallas kernels: 8.83 us -> 3.35 us  [local(): pl.pallas_call(functools.partial(lens, n_ord, cycles_here, fields), name=...]
    ppermute x6, waiting for transfers between devices: 8.09 us -> 4.36 us  [crossed(): lax.ppermute(x, axis, [(i, i ^ k) for i in range(n)])]
    pallas_call x1 -> x3, Pallas kernels: 5.54 us -> 6.44 us  [the longest x1 3.3 us: local(): pl.pallas_call(analysis, name='analysis', out_shape=pltpu.VMEM((cycles, w...]
    add x1, other arithmetic: 0.77 us -> 0.01 us  [local(): total = sum(crossed(part, 'band', n_band), own)]
    unnamed x8 -> x4, local copies, waits for them, and re-layouts: 0.6 us -> 0.01 us
    another operation x1 -> x0, other arithmetic: 0.56 us -> none  [local(): place = jnp.stack([band, slot]).astype(jnp.int32)]
  transfers between devices with their start and end apart: 6 -> 6, of which waited for: 5 -> 3; matrix products, arithmetic and copies ran while one was open for 0% -> 0% of each run, Pallas kernels for 0% -> 14%
where the time goes in v2:
time: 23 us; the launch traced here: 22.9 us
  Pallas kernels  9.79 us (43%)
  starting transfers between devices  7.99 us (35%)
  waiting for transfers between devices  4.36 us (19%)
  between operations  0.7 us (3%)
    ppermute x6, starting transfers between devices, crossed(): lax.ppermute(x, axis, [(i, i ^ k) for i in range(n)])  7.99 us
    ppermute x6, waiting for transfers between devices, crossed(): lax.ppermute(x, axis, [(i, i ^ k) for i in range(n)])  4.36 us
    pallas_call x1, Pallas kernels, local(): pl.pallas_call(functools.partial(lens, n_ord, cycles_here, fields), name=...  3.35 us
    pallas_call x1, Pallas kernels, local(): pl.pallas_call(analysis, name='analysis', out_shape=pltpu.VMEM((cycles, w...  3.3 us
    pallas_call x1, Pallas kernels, local(): pl.pallas_call(fetch, name='fetch', out_shape=(pltpu.VMEM(part.shape, par...  2.2 us
    pallas_call x1, Pallas kernels, local(): pl.pallas_call(functools.partial(near, n_ord, fields, npix_here), name='n...  0.95 us
  transfers between devices with their start and end apart: 6, of which 3 were waited for; matrix products, arithmetic and copies ran while one was open for 0% of the time, Pallas kernels for 14%

profile of v2, /device:TPU:0, one launch (start us, length us, event | category | flops | bytes accessed | tf_op | source)
XLA Modules:
  0.0 22.9 jit_solution(11685983468916145263)
XLA Ops:
  0.6 3.3 %analysis.1.part_ref = f32[16,512]{1,0:T(8,128)S(1)} custom-call(s32[4]{0:T(128)} %cycle_hbm.1, s32[1,64]{1,0:T(1,128)} %bitcast.3, bf16[16,64,2048]{2,1,0:T(8,128)(2,1)} %legendre_hbm.1, bf16[6,64,2048]{2,1,0:T(8,128)(2,1)} %alm_hbm.1), custom_call_target="tpu_custom_call" | custom-call | flops 2147483648 | bytes 6291456 | tf_op jit(solution)/shard_map/analysis/pallas_call | solution.py:251
  3.9 0.0 copy-start
  3.9 0.0 copy-start.1
  4.0 5.2 %collective-permute-start.2 = (f32[16,512]{1,0:T(8,128)S(1)}, f32[16,512]{1,0:T(8,128)S(1)}, u32[]{:S(2)}, u32[]{:S(2)}) collective-permute-start(f32[16,512]{1,0:T(8,128)S(1)} %analysis.1.part_ref), channel_id=1, source_target_pairs={{0,12},{4,8},{8,4},{12,0},{1,13},{5,9},{9,5},{13,1},{2,14},{6,10},... | collective-permute-start | bytes 98312 | tf_op jit(solution)/shard_map/ppermute | solution.py:230
  9.1 0.0 collective-permute-start.1
  9.1 0.6 %collective-permute-start = (f32[16,512]{1,0:T(8,128)S(1)}, f32[16,512]{1,0:T(8,128)S(1)}, u32[]{:S(2)}, u32[]{:S(2)}) collective-permute-start(f32[16,512]{1,0:T(8,128)S(1)} %analysis.1.part_ref), channel_id=1, source_target_pairs={{0,4},{4,0},{8,12},{12,8},{1,5},{5,1},{9,13},{13,9},{2,6},{6,2},{1... | collective-permute-start | bytes 98312 | tf_op jit(solution)/shard_map/ppermute | solution.py:230
  9.8 2.2 %fetch.1 = (f32[16,512]{1,0:T(8,128)S(1)}, bf16[128,128,128]{2,1,0:T(8,128)(2,1)S(1)}) custom-call(f32[16,512]{1,0:T(8,128)S(1)} %analysis.1.part_ref, bf16[128,128,128]{2,1,0:T(8,128)(2,1)} %weights_hbm.1), custom_call_target="tpu_custom_call" | custom-call | flops 1073741824 | bytes 6291456 | tf_op jit(solution)/shard_map/fetch/pallas_call | solution.py:267
  12.0 0.0 collective-permute-done.2
  12.0 2.0 %collective-permute-done.1 = f32[16,512]{1,0:T(8,128)S(1)} collective-permute-done((f32[16,512]{1,0:T(8,128)S(1)}, f32[16,512]{1,0:T(8,128)S(1)}, u32[]{:S(2)}, u32[]{:S(2)}) %collective-permute-start.1) | collective-permute-done | bytes 32800 | tf_op jit(solution)/shard_map/ppermute | solution.py:230
  13.9 0.0 collective-permute-done
  13.9 0.1 collective-permute-start.5
  14.0 1.6 %collective-permute-start.4 = (f32[16,512]{1,0:T(8,128)S(1)}, f32[16,512]{1,0:T(8,128)S(1)}, u32[]{:S(2)}, u32[]{:S(2)}) collective-permute-start(f32[16,512]{1,0:T(8,128)S(1)} %add_add_fusion.refs_0_), channel_id=1, source_target_pairs={{0,3},{1,2},{2,1},{3,0},{4,7},{5,6},{6,5},{7,4},{8,11},{9,10},{10,... | collective-permute-start | bytes 98312 | tf_op jit(solution)/shard_map/ppermute | solution.py:230
  15.6 0.6 %collective-permute-start.3 = (f32[16,512]{1,0:T(8,128)S(1)}, f32[16,512]{1,0:T(8,128)S(1)}, u32[]{:S(2)}, u32[]{:S(2)}) collective-permute-start(f32[16,512]{1,0:T(8,128)S(1)} %add_add_fusion.refs_0_), channel_id=1, source_target_pairs={{0,2},{1,3},{2,0},{3,1},{4,6},{5,7},{6,4},{7,5},{8,10},{9,11},{10,... | collective-permute-start | bytes 98312 | tf_op jit(solution)/shard_map/ppermute | solution.py:230
  16.2 0.0 collective-permute-done.5.refs_1_
  16.2 0.9 %near.1.refs_2_ = f32[384,512]{1,0:T(8,128)S(1)} custom-call(f32[16,512]{1,0:T(8,128)S(1)} %add_add_fusion.refs_0_, f32[16,512]{1,0:T(8,128)S(1)} %collective-permute-done.5.refs_1_), custom_call_target="tpu_custom_call" | custom-call | flops 1073741824 | bytes 1048576 | tf_op jit(solution)/shard_map/near/pallas_call | solution.py:282
  17.1 0.3 %collective-permute-done.4.refs_1_ = f32[16,512]{1,0:T(8,128)S(1)} collective-permute-done((f32[16,512]{1,0:T(8,128)S(1)}, f32[16,512]{1,0:T(8,128)S(1)}, u32[]{:S(2)}, u32[]{:S(2)}) %collective-permute-start.4) | collective-permute-done | bytes 32800 | tf_op jit(solution)/shard_map/ppermute | solution.py:230
  17.4 2.1 %collective-permute-done.3.refs_0_ = f32[16,512]{1,0:T(8,128)S(1)} collective-permute-done((f32[16,512]{1,0:T(8,128)S(1)}, f32[16,512]{1,0:T(8,128)S(1)}, u32[]{:S(2)}, u32[]{:S(2)}) %collective-permute-start.3) | collective-permute-done | bytes 32800 | tf_op jit(solution)/shard_map/ppermute | solution.py:230
  19.5 0.0 copy-done
  19.5 0.0 copy-done.1
  19.5 3.4 %lens.1 = (bf16[3,4,4096]{2,1,0:T(4,128)(2,1)}, f32[3,4,4096]{2,1,0:T(4,128)}) custom-call(s32[128]{0:T(128)S(1)} %bitcast.2, s32[128]{0:T(128)S(1)} %copy-done.1, f32[16,512]{1,0:T(8,128)S(1)} %collective-permute-done.3.refs_0_, f32[16,512]{1,0:T(8,128)S(1)} %collective-permute-done.4.refs_1_, f32[384,512]{1,0:T(8,128)S(1)} %near.1.refs_2_, ...), custom_call_target="tpu_custom_call" | custom-call | tf_op jit(solution)/shard_map/lens/pallas_call | solution.py:292
  (1 shorter events, 0.0 us)
Async XLA Ops:
  3.9 15.6 %copy-start = (s32[128,1]{0,1:T(1,128)S(1)}, s32[128,1]{0,1:T(1,128)}, u32[]{:S(2)}) copy-start(s32[128,1]{0,1:T(1,128)} %param.11) | copy-start | bytes 1540
  3.9 15.6 %copy-start.1 = (s32[128]{0:T(128)S(1)}, s32[128]{0:T(128)}, u32[]{:S(2)}) copy-start(s32[128]{0:T(128)} %src_block_ref.1) | copy-start | bytes 1540
  4.0 8.0 %collective-permute-start.2 = (f32[16,512]{1,0:T(8,128)S(1)}, f32[16,512]{1,0:T(8,128)S(1)}, u32[]{:S(2)}, u32[]{:S(2)}) collective-permute-start(f32[16,512]{1,0:T(8,128)S(1)} %analysis.1.part_ref), channel_id=1, source_target_pairs={{0,12},{4,8},{8,4},{12,0},{1,13},{5,9},{9,5},{13,1},{2,14},{6,10},... | collective-permute-start | bytes 98312 | tf_op jit(solution)/shard_map/ppermute | solution.py:230
  9.1 4.8 %collective-permute-start.1 = (f32[16,512]{1,0:T(8,128)S(1)}, f32[16,512]{1,0:T(8,128)S(1)}, u32[]{:S(2)}, u32[]{:S(2)}) collective-permute-start(f32[16,512]{1,0:T(8,128)S(1)} %analysis.1.part_ref), channel_id=1, source_target_pairs={{0,8},{4,12},{8,0},{12,4},{1,9},{5,13},{9,1},{13,5},{2,10},{6,14},... | collective-permute-start | bytes 98312 | tf_op jit(solution)/shard_map/ppermute | solution.py:230
  9.1 4.8 %collective-permute-start = (f32[16,512]{1,0:T(8,128)S(1)}, f32[16,512]{1,0:T(8,128)S(1)}, u32[]{:S(2)}, u32[]{:S(2)}) collective-permute-start(f32[16,512]{1,0:T(8,128)S(1)} %analysis.1.part_ref), channel_id=1, source_target_pairs={{0,4},{4,0},{8,12},{12,8},{1,5},{5,1},{9,13},{13,9},{2,6},{6,2},{1... | collective-permute-start | bytes 98312 | tf_op jit(solution)/shard_map/ppermute | solution.py:230
  13.9 2.2 %collective-permute-start.5 = (f32[16,512]{1,0:T(8,128)S(1)}, f32[16,512]{1,0:T(8,128)S(1)}, u32[]{:S(2)}, u32[]{:S(2)}) collective-permute-start(f32[16,512]{1,0:T(8,128)S(1)} %add_add_fusion.refs_0_), channel_id=1, source_target_pairs={{0,1},{1,0},{2,3},{3,2},{4,5},{5,4},{6,7},{7,6},{8,9},{9,8},{10,11... | collective-permute-start | bytes 98312 | tf_op jit(solution)/shard_map/ppermute | solution.py:230
  14.0 3.4 %collective-permute-start.4 = (f32[16,512]{1,0:T(8,128)S(1)}, f32[16,512]{1,0:T(8,128)S(1)}, u32[]{:S(2)}, u32[]{:S(2)}) collective-permute-start(f32[16,512]{1,0:T(8,128)S(1)} %add_add_fusion.refs_0_), channel_id=1, source_target_pairs={{0,3},{1,2},{2,1},{3,0},{4,7},{5,6},{6,5},{7,4},{8,11},{9,10},{10,... | collective-permute-start | bytes 98312 | tf_op jit(solution)/shard_map/ppermute | solution.py:230
  15.6 3.9 %collective-permute-start.3 = (f32[16,512]{1,0:T(8,128)S(1)}, f32[16,512]{1,0:T(8,128)S(1)}, u32[]{:S(2)}, u32[]{:S(2)}) collective-permute-start(f32[16,512]{1,0:T(8,128)S(1)} %add_add_fusion.refs_0_), channel_id=1, source_target_pairs={{0,2},{1,3},{2,0},{3,1},{4,6},{5,7},{6,4},{7,5},{8,10},{9,11},{10,... | collective-permute-start | bytes 98312 | tf_op jit(solution)/shard_map/ppermute | solution.py:230

commit v3 on v2

--- a/solution.py
+++ b/solution.py
@@ -1,5 +1,4 @@
 import functools
-import math
 
 import jax
 import jax.numpy as jnp
@@ -8,10 +7,12 @@
 from jax.experimental.pallas import tpu as pltpu
 from jax.sharding import PartitionSpec as P
 
+
 LANES = 128
 GROUP = 16
 Q_LEN = 512
 CHUNKS = 4
+UNROLL = 8
 NT = (((1,), (1,)), ((), ()))
 SINE = (6.2831851600887045, -41.34165503125142, 81.60100406374923, -76.54978209038376, 39.53670461908883)
 
@@ -96,11 +97,24 @@
         out_ref[:, 2 * f * orders : 2 * (f + 1) * orders] = jnp.concatenate(pieces, axis=1)
 
 
-def fetch(part_ref, weights_hbm, part_out, weights_ref, sem):
-    copy = pltpu.make_async_copy(weights_hbm, weights_ref, sem)
-    copy.start()
+def fetch(part_ref, weights_hbm, part_out, weights_ref, stage, sems):
+    count = weights_ref.shape[0] // CHUNKS
+    copies = [
+        pltpu.make_async_copy(
+            weights_hbm.at[pl.ds(i * count, count)], stage.at[pl.ds(i * count, count)], sems.at[i]
+        )
+        for i in range(CHUNKS)
+    ]
+    for copy in copies:
+        copy.start()
     part_out[...] = part_ref[...]
-    copy.wait()
+    for i, copy in enumerate(copies):
+        copy.wait()
+
+        @pl.loop(0, count, step=UNROLL)
+        def _(k):
+            for j in range(UNROLL):
+                weights_ref[i * count + k + j] = stage[i * count + k + j].T
 
 
 def synthesis(n_ord, fields, npix_here, arrays):
@@ -150,6 +164,9 @@
         columns.append(split(jnp.concatenate(rows, axis=0)))
     high, low_part = (jnp.concatenate(v, axis=1) for v in zip(*columns))
     dot = functools.partial(jnp.dot, preferred_element_type=jnp.float32)
+    if len(arrays) == 1:
+        both = jnp.concatenate([high, low_part], axis=1)
+        return dot(both, jnp.concatenate([table_high] * 2, axis=0)) + dot(high, table_low)
     return dot(high, table_high) + (dot(low_part, table_high) + dot(high, table_low))
 
 
@@ -157,9 +174,14 @@
     refs[-1][...] = synthesis(n_ord, fields, npix_here, [r[...] for r in refs[:-1]])
 
 
+def next_near(n_ord, fields, npix_here, array_ref, before_ref, out_ref):
+    out_ref[...] = before_ref[...] + synthesis(n_ord, fields, npix_here, [array_ref[...]])
+
+
 def lens(n_ord, cycles_here, fields, src_band_ref, src_block_ref, *refs):
-    arrays = refs[: n_ord // 2]
-    near_ref, weights, sky_hbm, lensed_hbm, sky, stage, sky_out, lensed_out, sems = refs[n_ord // 2 :]
+    last = n_ord // 2 - 1
+    arrays = refs[:last]
+    near_ref, weights, sky_hbm, lensed_hbm, sky, stage, sky_out, lensed_out, sems = refs[last:]
     band = lax.axis_index("band")
     cycles = arrays[0].shape[0]
     npix_here = sky_out.shape[2]
@@ -203,12 +225,12 @@
         left = jnp.concatenate([stage[2 * col], stage[2 * col + 1]], axis=1).astype(jnp.bfloat16)
         right = jnp.concatenate(
             [
-                jnp.concatenate([weights[c * cols + col], weights[(c + 1) * cols + col]], axis=1)
-                for c in range(0, cycles_here, 2)
+                jnp.concatenate([weights[c * cols + col] for c in range(n, cycles_here, 2)], axis=1)
+                for n in range(2)
             ],
             axis=0,
         )
-        full = lax.dot_general(left, right, NT, preferred_element_type=jnp.float32)
+        full = jnp.dot(left, right, preferred_element_type=jnp.float32)
         out = full[:, 0:LANES]
         for n in range(1, cycles_here // 2):
             out = jnp.where(cycle_of // 2 == n, full[:, n * LANES : (n + 1) * LANES], out)
@@ -227,7 +249,10 @@
 
 
 def crossed(x, axis, n):
-    return [lax.ppermute(x, axis, [(i, i ^ k) for i in range(n)]) for k in range(1, n)]
+    out = []
+    for k in range(1, n):
+        out.append(lax.ppermute(x, axis, [(i, i ^ k) for i in range(n)]))
+    return out
 
 
 def local(alm, legendre, order_ids, cycle_number, src_band, src_block, weights):
@@ -270,30 +295,40 @@
         out_shape=(pltpu.VMEM(part.shape, part.dtype), pltpu.VMEM(weights.shape, weights.dtype)),
         in_specs=[vmem, hbm],
         out_specs=(vmem, vmem),
-        scratch_shapes=[pltpu.SemaphoreType.DMA],
-        compiler_params=pltpu.CompilerParams(vmem_limit_bytes=8 << 20),
+        scratch_shapes=[pltpu.VMEM(weights.shape, weights.dtype), pltpu.SemaphoreType.DMA((CHUNKS,))],
+        compiler_params=pltpu.CompilerParams(vmem_limit_bytes=16 << 20),
         cost_estimate=pl.CostEstimate(flops=1 << 30, bytes_accessed=6 << 20, transcendentals=0),
     )(part, *far(weights))
     if n_band <= 8:
         total = sum(crossed(part, "band", n_band), own)
     else:
         total = lax.psum(own, "band")
-    arrays = [total] + crossed(total, "ord", n_ord)
-    first = pl.pallas_call(
-        functools.partial(near, n_ord, fields, npix_here),
-        name="near",
+
+    def swap(x, k):
+        return lax.ppermute(x, "ord", [(i, i ^ k) for i in range(n_ord)])
+
+    half = n_ord // 2
+    here = [total] + [swap(total, k) for k in range(1, half)]
+    there = swap(total, half)
+    rest = [swap(there, k) for k in range(1, half)]
+    synth = dict(
         out_shape=pltpu.VMEM((npix_here // q_len * fields * cycles, q_len), jnp.float32),
-        in_specs=[vmem] * (n_ord // 2),
         out_specs=vmem,
         compiler_params=pltpu.CompilerParams(vmem_limit_bytes=16 << 20),
         cost_estimate=pl.CostEstimate(flops=1 << 30, bytes_accessed=1 << 20, transcendentals=0),
-    )(*arrays[: n_ord // 2])
+    )
+    sums = pl.pallas_call(
+        functools.partial(near, n_ord, fields, npix_here), name="near", in_specs=[vmem] * half, **synth
+    )(*here)
+    sums = pl.pallas_call(
+        functools.partial(next_near, n_ord, fields, npix_here), name="next_near", in_specs=[vmem] * 2, **synth
+    )(there, sums)
     pixels = (fields, cycles_here, npix_here)
     return pl.pallas_call(
         functools.partial(lens, n_ord, cycles_here, fields),
         name="lens",
         out_shape=(jax.ShapeDtypeStruct(pixels, jnp.bfloat16), jax.ShapeDtypeStruct(pixels, jnp.float32)),
-        in_specs=[smem, smem] + [vmem] * (n_ord // 2 + 2),
+        in_specs=[smem, smem] + [vmem] * (half + 1),
         out_specs=(hbm, hbm),
         scratch_shapes=[
             pltpu.VMEM((cols * fields * cycles, blk), jnp.float32),
@@ -303,7 +338,7 @@
             pltpu.SemaphoreType.DMA((CHUNKS + 1,)),
         ],
         compiler_params=pltpu.CompilerParams(vmem_limit_bytes=32 << 20),
-    )(src_band[:, 0], src_block, *arrays[n_ord // 2 :], first, weights)
+    )(src_band[:, 0], src_block, *rest, sums, weights)
 
 
 def solution(mesh):

time: 23 us -> 23.3 us (1.013)
  Pallas kernels: 9.79 us -> 10.7 us
  starting transfers between devices: 7.99 us -> 7.32 us
    pallas_call x1, Pallas kernels: 2.2 us -> 3.22 us  [local(): pl.pallas_call(fetch, name='fetch', out_shape=(pltpu.VMEM(part.shape, par...]
    pallas_call x1, Pallas kernels: 3.35 us -> 2.55 us  [local(): pl.pallas_call(functools.partial(lens, n_ord, cycles_here, fields), name=...]
    ppermute x6, starting transfers between devices: 7.99 us -> 7.32 us  [the longest x3 5.72 us: crossed(): out.append(lax.ppermute(x, axis, [(i, i ^ k) for i in range(n)]))]
    pallas_call x0 -> x1, Pallas kernels: none -> 0.65 us  [local(): pl.pallas_call(functools.partial(next_near, n_ord, fields, npix_here), na...]
  transfers between devices with their start and end apart: 6 -> 6, of which waited for: 3 -> 3; matrix products, arithmetic and copies ran while one was open for 0% -> 0% of each run, Pallas kernels for 14% -> 21%
where the time goes in v3:
time: 23.3 us; the launch traced here: 23.2 us
  Pallas kernels  10.7 us (46%)
  starting transfers between devices  7.32 us (31%)
  waiting for transfers between devices  4.49 us (19%)
  between operations  0.71 us (3%)
    ppermute x3, starting transfers between devices, crossed(): out.append(lax.ppermute(x, axis, [(i, i ^ k) for i in range(n)]))  5.72 us
    pallas_call x1, Pallas kernels, local(): pl.pallas_call(analysis, name='analysis', out_shape=pltpu.VMEM((cycles, w...  3.3 us
    pallas_call x1, Pallas kernels, local(): pl.pallas_call(fetch, name='fetch', out_shape=(pltpu.VMEM(part.shape, par...  3.22 us
    pallas_call x1, Pallas kernels, local(): pl.pallas_call(functools.partial(lens, n_ord, cycles_here, fields), name=...  2.55 us
    ppermute x3, waiting for transfers between devices, crossed(): out.append(lax.ppermute(x, axis, [(i, i ^ k) for i in range(n)]))  2.44 us
    ppermute x3, waiting for transfers between devices, swap(): return lax.ppermute(x, 'ord', [(i, i ^ k) for i in range(n_ord)])  2.05 us
    ppermute x3, starting transfers between devices, swap(): return lax.ppermute(x, 'ord', [(i, i ^ k) for i in range(n_ord)])  1.6 us
    pallas_call x1, Pallas kernels, local(): pl.pallas_call(functools.partial(near, n_ord, fields, npix_here), name='n...  0.95 us
  transfers between devices with their start and end apart: 6, of which 3 were waited for; matrix products, arithmetic and copies ran while one was open for 0% of the time, Pallas kernels for 21%

profile of v3, /device:TPU:0, one launch (start us, length us, event | category | flops | bytes accessed | tf_op | source)
XLA Modules:
  0.0 23.2 jit_solution(12294628987859158956)
XLA Ops:
  0.6 3.3 %analysis.1.part_ref = f32[16,512]{1,0:T(8,128)S(1)} custom-call(s32[4]{0:T(128)} %cycle_hbm.1, s32[1,64]{1,0:T(1,128)} %bitcast.3, bf16[16,64,2048]{2,1,0:T(8,128)(2,1)} %legendre_hbm.1, bf16[6,64,2048]{2,1,0:T(8,128)(2,1)} %alm_hbm.1), custom_call_target="tpu_custom_call" | custom-call | flops 2147483648 | bytes 6291456 | tf_op jit(solution)/shard_map/analysis/pallas_call | solution.py:276
  3.9 3.1 %collective-permute-start = (f32[16,512]{1,0:T(8,128)S(1)}, f32[16,512]{1,0:T(8,128)S(1)}, u32[]{:S(2)}, u32[]{:S(2)}) collective-permute-start(f32[16,512]{1,0:T(8,128)S(1)} %analysis.1.part_ref), channel_id=1, source_target_pairs={{0,4},{4,0},{8,12},{12,8},{1,5},{5,1},{9,13},{13,9},{2,6},{6,2},{1... | collective-permute-start | bytes 98312 | tf_op jit(solution)/shard_map/ppermute | solution.py:254
  7.0 2.6 %collective-permute-start.1 = (f32[16,512]{1,0:T(8,128)S(1)}, f32[16,512]{1,0:T(8,128)S(1)}, u32[]{:S(2)}, u32[]{:S(2)}) collective-permute-start(f32[16,512]{1,0:T(8,128)S(1)} %analysis.1.part_ref), channel_id=1, source_target_pairs={{0,8},{4,12},{8,0},{12,4},{1,9},{5,13},{9,1},{13,5},{2,10},{6,14},... | collective-permute-start | bytes 98312 | tf_op jit(solution)/shard_map/ppermute | solution.py:254
  9.7 0.0 collective-permute-start.2
  9.7 3.2 %fetch.1 = (f32[16,512]{1,0:T(8,128)S(1)}, bf16[128,128,128]{2,1,0:T(8,128)(2,1)S(1)}) custom-call(f32[16,512]{1,0:T(8,128)S(1)} %analysis.1.part_ref, bf16[128,128,128]{2,1,0:T(8,128)(2,1)} %weights_hbm.1), custom_call_target="tpu_custom_call" | custom-call | flops 1073741824 | bytes 6291456 | tf_op jit(solution)/shard_map/fetch/pallas_call | solution.py:292
  12.9 0.0 copy-start
  12.9 0.0 copy-start.1
  12.9 0.0 collective-permute-done
  12.9 0.0 collective-permute-done.1
  12.9 2.4 %collective-permute-done.2 = f32[16,512]{1,0:T(8,128)S(1)} collective-permute-done((f32[16,512]{1,0:T(8,128)S(1)}, f32[16,512]{1,0:T(8,128)S(1)}, u32[]{:S(2)}, u32[]{:S(2)}) %collective-permute-start.2) | collective-permute-done | bytes 32800 | tf_op jit(solution)/shard_map/ppermute | solution.py:254
  15.4 0.1 collective-permute-start.5
  15.5 1.5 %collective-permute-start.3 = (f32[16,512]{1,0:T(8,128)S(1)}, f32[16,512]{1,0:T(8,128)S(1)}, u32[]{:S(2)}, u32[]{:S(2)}) collective-permute-start(f32[16,512]{1,0:T(8,128)S(1)} %add_add_fusion.refs_0_), channel_id=1, source_target_pairs={{0,2},{1,3},{2,0},{3,1},{4,6},{5,7},{6,4},{7,5},{8,10},{9,11},{10,... | collective-permute-start | bytes 98312 | tf_op jit(solution)/shard_map/ppermute | solution.py:308
  17.0 0.0 collective-permute-done.5.refs_1_
  17.0 0.9 %near.1.before_ref = f32[384,512]{1,0:T(8,128)S(1)} custom-call(f32[16,512]{1,0:T(8,128)S(1)} %add_add_fusion.refs_0_, f32[16,512]{1,0:T(8,128)S(1)} %collective-permute-done.5.refs_1_), custom_call_target="tpu_custom_call" | custom-call | flops 1073741824 | bytes 1048576 | tf_op jit(solution)/shard_map/near/pallas_call | solution.py:320
  17.9 1.5 %collective-permute-done.3.array_ref = f32[16,512]{1,0:T(8,128)S(1)} collective-permute-done((f32[16,512]{1,0:T(8,128)S(1)}, f32[16,512]{1,0:T(8,128)S(1)}, u32[]{:S(2)}, u32[]{:S(2)}) %collective-permute-start.3) | collective-permute-done | bytes 32800 | tf_op jit(solution)/shard_map/ppermute | solution.py:308
  19.4 0.0 collective-permute-start.4
  19.4 0.6 %next_near.1.refs_1_ = f32[384,512]{1,0:T(8,128)S(1)} custom-call(f32[16,512]{1,0:T(8,128)S(1)} %collective-permute-done.3.array_ref, f32[384,512]{1,0:T(8,128)S(1)} %near.1.before_ref), custom_call_target="tpu_custom_call" | custom-call | flops 1073741824 | bytes 1048576 | tf_op jit(solution)/shard_map/next_near/pallas_call | solution.py:323
  20.1 0.5 %collective-permute-done.4.refs_0_ = f32[16,512]{1,0:T(8,128)S(1)} collective-permute-done((f32[16,512]{1,0:T(8,128)S(1)}, f32[16,512]{1,0:T(8,128)S(1)}, u32[]{:S(2)}, u32[]{:S(2)}) %collective-permute-start.4) | collective-permute-done | bytes 32800 | tf_op jit(solution)/shard_map/ppermute | solution.py:308
  20.6 0.0 copy-done
  20.6 0.0 copy-done.1
  20.7 2.5 %lens.1 = (bf16[3,4,4096]{2,1,0:T(4,128)(2,1)}, f32[3,4,4096]{2,1,0:T(4,128)}) custom-call(s32[128]{0:T(128)S(1)} %bitcast.2, s32[128]{0:T(128)S(1)} %copy-done.1, f32[16,512]{1,0:T(8,128)S(1)} %collective-permute-done.4.refs_0_, f32[384,512]{1,0:T(8,128)S(1)} %next_near.1.refs_1_, bf16[128,128,128]{2,1,0:T(8,128)(2,1)S(1)} %get-tuple-element.5.refs_2_), custom_call_target="tpu_custom_call" | custom-call | tf_op jit(solution)/shard_map/lens/pallas_call | solution.py:327
  (1 shorter events, 0.0 us)
Async XLA Ops:
  3.9 9.0 %collective-permute-start = (f32[16,512]{1,0:T(8,128)S(1)}, f32[16,512]{1,0:T(8,128)S(1)}, u32[]{:S(2)}, u32[]{:S(2)}) collective-permute-start(f32[16,512]{1,0:T(8,128)S(1)} %analysis.1.part_ref), channel_id=1, source_target_pairs={{0,4},{4,0},{8,12},{12,8},{1,5},{5,1},{9,13},{13,9},{2,6},{6,2},{1... | collective-permute-start | bytes 98312 | tf_op jit(solution)/shard_map/ppermute | solution.py:254
  7.0 5.9 %collective-permute-start.1 = (f32[16,512]{1,0:T(8,128)S(1)}, f32[16,512]{1,0:T(8,128)S(1)}, u32[]{:S(2)}, u32[]{:S(2)}) collective-permute-start(f32[16,512]{1,0:T(8,128)S(1)} %analysis.1.part_ref), channel_id=1, source_target_pairs={{0,8},{4,12},{8,0},{12,4},{1,9},{5,13},{9,1},{13,5},{2,10},{6,14},... | collective-permute-start | bytes 98312 | tf_op jit(solution)/shard_map/ppermute | solution.py:254
  9.7 5.7 %collective-permute-start.2 = (f32[16,512]{1,0:T(8,128)S(1)}, f32[16,512]{1,0:T(8,128)S(1)}, u32[]{:S(2)}, u32[]{:S(2)}) collective-permute-start(f32[16,512]{1,0:T(8,128)S(1)} %analysis.1.part_ref), channel_id=1, source_target_pairs={{0,12},{4,8},{8,4},{12,0},{1,13},{5,9},{9,5},{13,1},{2,14},{6,10},... | collective-permute-start | bytes 98312 | tf_op jit(solution)/shard_map/ppermute | solution.py:254
  12.9 7.8 %copy-start = (s32[128,1]{0,1:T(1,128)S(1)}, s32[128,1]{0,1:T(1,128)}, u32[]{:S(2)}) copy-start(s32[128,1]{0,1:T(1,128)} %param.11) | copy-start | bytes 1540
  12.9 7.8 %copy-start.1 = (s32[128]{0:T(128)S(1)}, s32[128]{0:T(128)}, u32[]{:S(2)}) copy-start(s32[128]{0:T(128)} %src_block_ref.1) | copy-start | bytes 1540
  15.4 1.6 %collective-permute-start.5 = (f32[16,512]{1,0:T(8,128)S(1)}, f32[16,512]{1,0:T(8,128)S(1)}, u32[]{:S(2)}, u32[]{:S(2)}) collective-permute-start(f32[16,512]{1,0:T(8,128)S(1)} %add_add_fusion.refs_0_), channel_id=1, source_target_pairs={{0,1},{1,0},{2,3},{3,2},{4,5},{5,4},{6,7},{7,6},{8,9},{9,8},{10,11... | collective-permute-start | bytes 98312 | tf_op jit(solution)/shard_map/ppermute | solution.py:308
  15.5 4.0 %collective-permute-start.3 = (f32[16,512]{1,0:T(8,128)S(1)}, f32[16,512]{1,0:T(8,128)S(1)}, u32[]{:S(2)}, u32[]{:S(2)}) collective-permute-start(f32[16,512]{1,0:T(8,128)S(1)} %add_add_fusion.refs_0_), channel_id=1, source_target_pairs={{0,2},{1,3},{2,0},{3,1},{4,6},{5,7},{6,4},{7,5},{8,10},{9,11},{10,... | collective-permute-start | bytes 98312 | tf_op jit(solution)/shard_map/ppermute | solution.py:308
  19.4 1.2 %collective-permute-start.4 = (f32[16,512]{1,0:T(8,128)S(1)}, f32[16,512]{1,0:T(8,128)S(1)}, u32[]{:S(2)}, u32[]{:S(2)}) collective-permute-start(f32[16,512]{1,0:T(8,128)S(1)} %collective-permute-done.3.array_ref), channel_id=1, source_target_pairs={{0,1},{1,0},{2,3},{3,2},{4,5},{5,4},{6,7},{7,6},{8,9},{9,8},{10,11... | collective-permute-start | bytes 98312 | tf_op jit(solution)/shard_map/ppermute | solution.py:308

commit v4 on v3

--- a/solution.py
+++ b/solution.py
@@ -13,6 +13,7 @@
 Q_LEN = 512
 CHUNKS = 4
 UNROLL = 8
+META = 8
 NT = (((1,), (1,)), ((), ()))
 SINE = (6.2831851600887045, -41.34165503125142, 81.60100406374923, -76.54978209038376, 39.53670461908883)
 
@@ -64,15 +65,16 @@
         copy.wait()
     band = lax.axis_index("band")
     cycles_here = cycle_ref.shape[0]
-    row = lax.broadcasted_iota(jnp.int32, (cycles, LANES // 2), 0)
-    parity = jnp.zeros((cycles, LANES // 2), jnp.float32)
+    lane = lax.broadcasted_iota(jnp.int32, (1, LANES), 1)
+    parity = jnp.zeros((1, LANES), jnp.float32)
     for i in range(cycles_here):
         odd = (cycle_ref[i] & 1).astype(jnp.float32)
-        parity = jnp.where(row == band * cycles_here + i, odd, parity)
+        parity = jnp.where(lane == band * cycles_here + i, odd, parity)
     ids = orders_ref[...].astype(jnp.float32) * jnp.where(band == 0, 1.0, 0.0)
-    base = half * 2 * orders
-    out_ref[:, base : base + orders] = jnp.broadcast_to(ids, (cycles, orders))
-    out_ref[:, base + orders : base + 2 * orders] = parity
+    base = half * cycles
+    out_ref[base : base + 1, :] = jnp.concatenate([ids, ids], axis=1)
+    out_ref[base + 1 : base + 2, :] = parity
+    out_ref[base + 2 :, :] = jnp.zeros((META - 2, LANES), jnp.float32)
 
     width = parts * GROUP
     share = cycles // 2
@@ -94,10 +96,10 @@
         sums.append(jnp.concatenate(both, axis=0))
     for f in range(half):
         pieces = [sums[g][:, c * GROUP : (c + 1) * GROUP] for c in (f, f + half) for g in range(groups)]
-        out_ref[:, 2 * f * orders : 2 * (f + 1) * orders] = jnp.concatenate(pieces, axis=1)
-
-
-def fetch(part_ref, weights_hbm, part_out, weights_ref, stage, sems):
+        out_ref[f * cycles : (f + 1) * cycles, :] = jnp.concatenate(pieces, axis=1)
+
+
+def fetch(cycles_here, rows_col, cols, part_ref, src_band_ref, src_block_ref, weights_hbm, part_out, places_ref, weights_ref, stage, sems):
     count = weights_ref.shape[0] // CHUNKS
     copies = [
         pltpu.make_async_copy(
@@ -108,6 +110,9 @@
     for copy in copies:
         copy.start()
     part_out[...] = part_ref[...]
+    block = src_block_ref[...]
+    cycle = src_band_ref[...] * cycles_here + lax.shift_right_logical(block, cols.bit_length() - 1)
+    places_ref[...] = (block & (cols - 1)) * rows_col + cycle
     for i, copy in enumerate(copies):
         copy.wait()
 
@@ -119,18 +124,15 @@
 
 def synthesis(n_ord, fields, npix_here, arrays):
     slot = lax.axis_index("ord").astype(jnp.float32)
-    cycles = arrays[0].shape[0]
+    base = arrays[0].shape[0] - META
+    cycles = base // fields
     half = LANES // 2
     npix = npix_here * n_ord
     q_len = min(Q_LEN, npix_here)
     p_len = npix_here // q_len
 
-    lane = lax.broadcasted_iota(jnp.int32, (cycles, LANES), 1)
-    low = lane < half
-    low_row = low[0:1]
-    meta = [a[:, fields * LANES :] for a in arrays]
-    ids = [jnp.where(low_row, m[0:1], pltpu.roll(m, half, 1)[0:1]) for m in meta]
-    odd = jnp.where(low, pltpu.roll(meta[0], half, 1), meta[0]) > 0.5
+    ids = [a[base : base + 1] for a in arrays]
+    odd = jnp.broadcast_to(arrays[0][base + 1 : base + 2], (LANES, LANES)).T[:cycles] > 0.5
 
     q_iota = lax.broadcasted_iota(jnp.int32, (LANES, q_len), 1).astype(jnp.float32) * (1.0 / npix)
     shift = jnp.where(lax.broadcasted_iota(jnp.int32, (LANES, q_len), 0) < half, 0.0, 0.25)
@@ -154,7 +156,7 @@
             cosine = cos_turns(turn) * factor
             sine = cos_turns(wrap(turn - 0.25)) * factor
             terms.append((jnp.where(low_p, cosine, -cosine), -sine))
-        x = [a[:, f * LANES : (f + 1) * LANES] for f in range(fields)]
+        x = [a[f * cycles : (f + 1) * cycles] for f in range(fields)]
         crossed_x = [pltpu.roll(v, half, 1) for v in x]
         rows = []
         for p in range(p_len):
@@ -178,12 +180,14 @@
     out_ref[...] = before_ref[...] + synthesis(n_ord, fields, npix_here, [array_ref[...]])
 
 
-def lens(n_ord, cycles_here, fields, src_band_ref, src_block_ref, *refs):
+def lens(n_ord, cycles_here, fields, places_vmem, *refs):
     last = n_ord // 2 - 1
     arrays = refs[:last]
-    near_ref, weights, sky_hbm, lensed_hbm, sky, stage, sky_out, lensed_out, sems = refs[last:]
+    near_ref, weights, sky_hbm, lensed_hbm, sky, stage, sky_out, lensed_out, places, sems = refs[last:]
+    listing = pltpu.make_async_copy(places_vmem, places, sems.at[CHUNKS + 1])
+    listing.start()
     band = lax.axis_index("band")
-    cycles = arrays[0].shape[0]
+    cycles = (arrays[0].shape[0] - META) // fields
     npix_here = sky_out.shape[2]
     cols = npix_here // LANES
     q_len = near_ref.shape[1]
@@ -207,15 +211,11 @@
     copies = [pltpu.make_async_copy(sky_out, sky_hbm, sems.at[0])]
     copies[0].start()
 
-    shift_bits = cols.bit_length() - 1
+    listing.wait()
     stage[...] = jnp.zeros_like(stage)
     for col in range(cols):
         for c in range(cycles_here):
-            k = c * cols + col
-            block = src_block_ref[k]
-            cycle = src_band_ref[k] * cycles_here + lax.shift_right_logical(block, shift_bits)
-            begin = (block & (cols - 1)) * rows_col + cycle
-            source = sky[pl.ds(begin, fields, stride=cycles), :]
+            source = sky[pl.ds(places[0, c * cols + col], fields, stride=cycles), :]
             stage[2 * col + c % 2, pl.ds(c, fields, stride=cycles_here), :] = source
 
     rows = stage.shape[1]
@@ -263,10 +263,9 @@
     cycles_here = cycle_number.shape[0]
     blocks, blk, _ = weights.shape
     npix_here = blocks * blk // cycles_here
-    width = (fields + 1) * 2 * orders
+    message = (fields * cycles + META, 2 * orders)
     cols = npix_here // blk
     q_len = min(Q_LEN, npix_here)
-    smem = pl.BlockSpec(memory_space=pltpu.SMEM)
     vmem = pl.BlockSpec(memory_space=pltpu.VMEM)
     hbm = pl.BlockSpec(memory_space=pltpu.HBM)
 
@@ -276,7 +275,7 @@
     part = pl.pallas_call(
         analysis,
         name="analysis",
-        out_shape=pltpu.VMEM((cycles, width), jnp.float32),
+        out_shape=pltpu.VMEM(message, jnp.float32),
         in_specs=[hbm] * 4,
         out_specs=vmem,
         scratch_shapes=[
@@ -289,16 +288,20 @@
         compiler_params=pltpu.CompilerParams(vmem_limit_bytes=16 << 20),
         cost_estimate=pl.CostEstimate(flops=2 << 30, bytes_accessed=6 << 20, transcendentals=0),
     )(*far(cycle_number, order_ids[None], legendre, alm))
-    own, weights = pl.pallas_call(
-        fetch,
+    own, places, weights = pl.pallas_call(
+        functools.partial(fetch, cycles_here, fields * cycles, cols),
         name="fetch",
-        out_shape=(pltpu.VMEM(part.shape, part.dtype), pltpu.VMEM(weights.shape, weights.dtype)),
-        in_specs=[vmem, hbm],
-        out_specs=(vmem, vmem),
+        out_shape=(
+            pltpu.VMEM(part.shape, part.dtype),
+            pltpu.VMEM((1, blocks), jnp.int32),
+            pltpu.VMEM(weights.shape, weights.dtype),
+        ),
+        in_specs=[vmem, vmem, vmem, hbm],
+        out_specs=(vmem, vmem, vmem),
         scratch_shapes=[pltpu.VMEM(weights.shape, weights.dtype), pltpu.SemaphoreType.DMA((CHUNKS,))],
         compiler_params=pltpu.CompilerParams(vmem_limit_bytes=16 << 20),
         cost_estimate=pl.CostEstimate(flops=1 << 30, bytes_accessed=6 << 20, transcendentals=0),
-    )(part, *far(weights))
+    )(part, src_band.T, src_block[None], *far(weights))
     if n_band <= 8:
         total = sum(crossed(part, "band", n_band), own)
     else:
@@ -328,17 +331,18 @@
         functools.partial(lens, n_ord, cycles_here, fields),
         name="lens",
         out_shape=(jax.ShapeDtypeStruct(pixels, jnp.bfloat16), jax.ShapeDtypeStruct(pixels, jnp.float32)),
-        in_specs=[smem, smem] + [vmem] * (half + 1),
+        in_specs=[vmem] * (half + 2),
         out_specs=(hbm, hbm),
         scratch_shapes=[
             pltpu.VMEM((cols * fields * cycles, blk), jnp.float32),
             pltpu.VMEM((2 * cols, 16, blk), jnp.float32),
             pltpu.VMEM(pixels, jnp.bfloat16),
             pltpu.VMEM(pixels, jnp.float32),
-            pltpu.SemaphoreType.DMA((CHUNKS + 1,)),
+            pltpu.SMEM((1, blocks), jnp.int32),
+            pltpu.SemaphoreType.DMA((CHUNKS + 2,)),
         ],
         compiler_params=pltpu.CompilerParams(vmem_limit_bytes=32 << 20),
-    )(src_band[:, 0], src_block, *rest, sums, weights)
+    )(places, *rest, sums, weights)
 
 
 def solution(mesh):

time: 23.3 us -> 22.8 us (0.979)
  Pallas kernels: 10.7 us -> 10.1 us
    pallas_call x1, Pallas kernels: 2.55 us -> 2.08 us  [local(): pl.pallas_call(functools.partial(lens, n_ord, cycles_here, fields), name=...]
where the time goes in v4:
time: 22.8 us; the launch traced here: 22.6 us
  Pallas kernels  10.1 us (44%)
  starting transfers between devices  7.35 us (32%)
  waiting for transfers between devices  4.48 us (20%)
  between operations  0.71 us (3%)
    ppermute x3, starting transfers between devices, crossed(): out.append(lax.ppermute(x, axis, [(i, i ^ k) for i in range(n)]))  5.71 us
    pallas_call x1, Pallas kernels, local(): pl.pallas_call(analysis, name='analysis', out_shape=pltpu.VMEM(message, j...  3.28 us
    pallas_call x1, Pallas kernels, local(): pl.pallas_call(functools.partial(fetch, cycles_here, fields * cycles, col...  3.22 us
    ppermute x3, waiting for transfers between devices, crossed(): out.append(lax.ppermute(x, axis, [(i, i ^ k) for i in range(n)]))  2.41 us
    pallas_call x1, Pallas kernels, local(): pl.pallas_call(functools.partial(lens, n_ord, cycles_here, fields), name=...  2.08 us
    ppermute x3, waiting for transfers between devices, swap(): return lax.ppermute(x, 'ord', [(i, i ^ k) for i in range(n_ord)])  2.07 us
    ppermute x3, starting transfers between devices, swap(): return lax.ppermute(x, 'ord', [(i, i ^ k) for i in range(n_ord)])  1.64 us
    pallas_call x1, Pallas kernels, local(): pl.pallas_call(functools.partial(near, n_ord, fields, npix_here), name='n...  0.89 us
  transfers between devices with their start and end apart: 6, of which 3 were waited for; matrix products, arithmetic and copies ran while one was open for 0% of the time, Pallas kernels for 21%

profile of v4, /device:TPU:0, one launch (start us, length us, event | category | flops | bytes accessed | tf_op | source)
XLA Modules:
  0.0 22.6 jit_solution(17647642951955661336)
XLA Ops:
  0.6 0.0 copy-start
  0.6 0.0 copy-start.1
  0.7 3.3 %analysis.1.part_ref = f32[56,128]{1,0:T(8,128)S(1)} custom-call(s32[4]{0:T(128)} %cycle_hbm.1, s32[1,64]{1,0:T(1,128)} %bitcast.5, bf16[16,64,2048]{2,1,0:T(8,128)(2,1)} %legendre_hbm.1, bf16[6,64,2048]{2,1,0:T(8,128)(2,1)} %alm_hbm.1), custom_call_target="tpu_custom_call" | custom-call | flops 2147483648 | bytes 6291456 | tf_op jit(solution)/shard_map/analysis/pallas_call | solution.py:275
  3.9 3.1 %collective-permute-start = (f32[56,128]{1,0:T(8,128)S(1)}, f32[56,128]{1,0:T(8,128)S(1)}, u32[]{:S(2)}, u32[]{:S(2)}) collective-permute-start(f32[56,128]{1,0:T(8,128)S(1)} %analysis.1.part_ref), channel_id=1, source_target_pairs={{0,4},{4,0},{8,12},{12,8},{1,5},{5,1},{9,13},{13,9},{2,6},{6,2},{1... | collective-permute-start | bytes 86024 | tf_op jit(solution)/shard_map/ppermute | solution.py:254
  7.1 2.6 %collective-permute-start.1 = (f32[56,128]{1,0:T(8,128)S(1)}, f32[56,128]{1,0:T(8,128)S(1)}, u32[]{:S(2)}, u32[]{:S(2)}) collective-permute-start(f32[56,128]{1,0:T(8,128)S(1)} %analysis.1.part_ref), channel_id=1, source_target_pairs={{0,8},{4,12},{8,0},{12,4},{1,9},{5,13},{9,1},{13,5},{2,10},{6,14},... | collective-permute-start | bytes 86024 | tf_op jit(solution)/shard_map/ppermute | solution.py:254
  9.7 0.0 collective-permute-start.2
  9.7 0.0 copy-done
  9.7 0.0 copy-done.1
  9.7 3.2 %fetch.1 = (f32[56,128]{1,0:T(8,128)S(1)}, s32[1,128]{1,0:T(1,128)S(1)}, bf16[128,128,128]{2,1,0:T(8,128)(2,1)S(1)}) custom-call(f32[56,128]{1,0:T(8,128)S(1)} %analysis.1.part_ref, s32[1,128]{1,0:T(1,128)S(1)} %bitcast.3, s32[1,128]{1,0:T(1,128)S(1)} %bitcast.4, bf16[128,128,128]{2,1,0:T(8,128)(2,1)} %weights_hbm.1), custom_call_target="tpu_custom_call" | custom-call | flops 1073741824 | bytes 6291456 | tf_op jit(solution)/shard_map/fetch/pallas_call | solution.py:291
  12.9 0.0 collective-permute-done
  12.9 0.0 collective-permute-done.1
  12.9 2.4 %collective-permute-done.2 = f32[56,128]{1,0:T(8,128)S(1)} collective-permute-done((f32[56,128]{1,0:T(8,128)S(1)}, f32[56,128]{1,0:T(8,128)S(1)}, u32[]{:S(2)}, u32[]{:S(2)}) %collective-permute-start.2) | collective-permute-done | bytes 28704 | tf_op jit(solution)/shard_map/ppermute | solution.py:254
  15.3 0.1 collective-permute-start.5
  15.4 1.6 %collective-permute-start.3 = (f32[56,128]{1,0:T(8,128)S(1)}, f32[56,128]{1,0:T(8,128)S(1)}, u32[]{:S(2)}, u32[]{:S(2)}) collective-permute-start(f32[56,128]{1,0:T(8,128)S(1)} %add_add_fusion.refs_0_), channel_id=1, source_target_pairs={{0,2},{1,3},{2,0},{3,1},{4,6},{5,7},{6,4},{7,5},{8,10},{9,11},{10,... | collective-permute-start | bytes 86024 | tf_op jit(solution)/shard_map/ppermute | solution.py:311
  17.0 0.0 collective-permute-done.5.refs_1_
  17.0 0.9 %near.1.before_ref = f32[384,512]{1,0:T(8,128)S(1)} custom-call(f32[56,128]{1,0:T(8,128)S(1)} %add_add_fusion.refs_0_, f32[56,128]{1,0:T(8,128)S(1)} %collective-permute-done.5.refs_1_), custom_call_target="tpu_custom_call" | custom-call | flops 1073741824 | bytes 1048576 | tf_op jit(solution)/shard_map/near/pallas_call | solution.py:323
  17.9 1.5 %collective-permute-done.3.array_ref = f32[56,128]{1,0:T(8,128)S(1)} collective-permute-done((f32[56,128]{1,0:T(8,128)S(1)}, f32[56,128]{1,0:T(8,128)S(1)}, u32[]{:S(2)}, u32[]{:S(2)}) %collective-permute-start.3) | collective-permute-done | bytes 28704 | tf_op jit(solution)/shard_map/ppermute | solution.py:311
  19.3 0.0 collective-permute-start.4
  19.4 0.6 %next_near.1.refs_1_ = f32[384,512]{1,0:T(8,128)S(1)} custom-call(f32[56,128]{1,0:T(8,128)S(1)} %collective-permute-done.3.array_ref, f32[384,512]{1,0:T(8,128)S(1)} %near.1.before_ref), custom_call_target="tpu_custom_call" | custom-call | flops 1073741824 | bytes 1048576 | tf_op jit(solution)/shard_map/next_near/pallas_call | solution.py:326
  20.0 0.6 %collective-permute-done.4.refs_0_ = f32[56,128]{1,0:T(8,128)S(1)} collective-permute-done((f32[56,128]{1,0:T(8,128)S(1)}, f32[56,128]{1,0:T(8,128)S(1)}, u32[]{:S(2)}, u32[]{:S(2)}) %collective-permute-start.4) | collective-permute-done | bytes 28704 | tf_op jit(solution)/shard_map/ppermute | solution.py:311
  20.6 2.1 %lens.1 = (bf16[3,4,4096]{2,1,0:T(4,128)(2,1)}, f32[3,4,4096]{2,1,0:T(4,128)}) custom-call(s32[1,128]{1,0:T(1,128)S(1)} %get-tuple-element.5.places_vmem, f32[56,128]{1,0:T(8,128)S(1)} %collective-permute-done.4.refs_0_, f32[384,512]{1,0:T(8,128)S(1)} %next_near.1.refs_1_, bf16[128,128,128]{2,1,0:T(8,128)(2,1)S(1)} %get-tuple-element.7.refs_2_), custom_call_target="tpu_custom_call" | custom-call | tf_op jit(solution)/shard_map/lens/pallas_call | solution.py:330
  (1 shorter events, 0.0 us)
Async XLA Ops:
  0.6 9.0 %copy-start = (s32[128,1]{0,1:T(1,128)S(1)}, s32[128,1]{0,1:T(1,128)}, u32[]{:S(2)}) copy-start(s32[128,1]{0,1:T(1,128)} %param.11) | copy-start | bytes 1540
  0.6 9.0 %copy-start.1 = (s32[128]{0:T(128)S(1)}, s32[128]{0:T(128)}, u32[]{:S(2)}) copy-start(s32[128]{0:T(128)} %param.12) | copy-start | bytes 1540
  3.9 9.0 %collective-permute-start = (f32[56,128]{1,0:T(8,128)S(1)}, f32[56,128]{1,0:T(8,128)S(1)}, u32[]{:S(2)}, u32[]{:S(2)}) collective-permute-start(f32[56,128]{1,0:T(8,128)S(1)} %analysis.1.part_ref), channel_id=1, source_target_pairs={{0,4},{4,0},{8,12},{12,8},{1,5},{5,1},{9,13},{13,9},{2,6},{6,2},{1... | collective-permute-start | bytes 86024 | tf_op jit(solution)/shard_map/ppermute | solution.py:254
  7.1 5.8 %collective-permute-start.1 = (f32[56,128]{1,0:T(8,128)S(1)}, f32[56,128]{1,0:T(8,128)S(1)}, u32[]{:S(2)}, u32[]{:S(2)}) collective-permute-start(f32[56,128]{1,0:T(8,128)S(1)} %analysis.1.part_ref), channel_id=1, source_target_pairs={{0,8},{4,12},{8,0},{12,4},{1,9},{5,13},{9,1},{13,5},{2,10},{6,14},... | collective-permute-start | bytes 86024 | tf_op jit(solution)/shard_map/ppermute | solution.py:254
  9.7 5.7 %collective-permute-start.2 = (f32[56,128]{1,0:T(8,128)S(1)}, f32[56,128]{1,0:T(8,128)S(1)}, u32[]{:S(2)}, u32[]{:S(2)}) collective-permute-start(f32[56,128]{1,0:T(8,128)S(1)} %analysis.1.part_ref), channel_id=1, source_target_pairs={{0,12},{4,8},{8,4},{12,0},{1,13},{5,9},{9,5},{13,1},{2,14},{6,10},... | collective-permute-start | bytes 86024 | tf_op jit(solution)/shard_map/ppermute | solution.py:254
  15.3 1.6 %collective-permute-start.5 = (f32[56,128]{1,0:T(8,128)S(1)}, f32[56,128]{1,0:T(8,128)S(1)}, u32[]{:S(2)}, u32[]{:S(2)}) collective-permute-start(f32[56,128]{1,0:T(8,128)S(1)} %add_add_fusion.refs_0_), channel_id=1, source_target_pairs={{0,1},{1,0},{2,3},{3,2},{4,5},{5,4},{6,7},{7,6},{8,9},{9,8},{10,11... | collective-permute-start | bytes 86024 | tf_op jit(solution)/shard_map/ppermute | solution.py:311
  15.4 3.9 %collective-permute-start.3 = (f32[56,128]{1,0:T(8,128)S(1)}, f32[56,128]{1,0:T(8,128)S(1)}, u32[]{:S(2)}, u32[]{:S(2)}) collective-permute-start(f32[56,128]{1,0:T(8,128)S(1)} %add_add_fusion.refs_0_), channel_id=1, source_target_pairs={{0,2},{1,3},{2,0},{3,1},{4,6},{5,7},{6,4},{7,5},{8,10},{9,11},{10,... | collective-permute-start | bytes 86024 | tf_op jit(solution)/shard_map/ppermute | solution.py:311
  19.3 1.2 %collective-permute-start.4 = (f32[56,128]{1,0:T(8,128)S(1)}, f32[56,128]{1,0:T(8,128)S(1)}, u32[]{:S(2)}, u32[]{:S(2)}) collective-permute-start(f32[56,128]{1,0:T(8,128)S(1)} %collective-permute-done.3.array_ref), channel_id=1, source_target_pairs={{0,1},{1,0},{2,3},{3,2},{4,5},{5,4},{6,7},{7,6},{8,9},{9,8},{10,11... | collective-permute-start | bytes 86024 | tf_op jit(solution)/shard_map/ppermute | solution.py:311

commit v5 on v4

--- a/solution.py
+++ b/solution.py
@@ -12,7 +12,7 @@
 GROUP = 16
 Q_LEN = 512
 CHUNKS = 4
-UNROLL = 8
+UNROLL = 32
 META = 8
 NT = (((1,), (1,)), ((), ()))
 SINE = (6.2831851600887045, -41.34165503125142, 81.60100406374923, -76.54978209038376, 39.53670461908883)
@@ -248,10 +248,10 @@
         copy.wait()
 
 
-def crossed(x, axis, n):
+def shifted(x, axis, n):
     out = []
     for k in range(1, n):
-        out.append(lax.ppermute(x, axis, [(i, i ^ k) for i in range(n)]))
+        out.append(lax.ppermute(x, axis, [(i, (i + k) % n) for i in range(n)]))
     return out
 
 
@@ -303,7 +303,7 @@
         cost_estimate=pl.CostEstimate(flops=1 << 30, bytes_accessed=6 << 20, transcendentals=0),
     )(part, src_band.T, src_block[None], *far(weights))
     if n_band <= 8:
-        total = sum(crossed(part, "band", n_band), own)
+        total = sum(shifted(part, "band", n_band), own)
     else:
         total = lax.psum(own, "band")
 

time: 22.8 us -> 21.1 us (0.925)
  waiting for transfers between devices: 4.48 us -> 2.08 us
  starting transfers between devices: 7.35 us -> 8.68 us
  Pallas kernels: 10.1 us -> 9.41 us
    ppermute x3, waiting for transfers between devices: 2.41 us -> 0.01 us  [shifted(): out.append(lax.ppermute(x, axis, [(i, (i + k) % n) for i in range(n)]))]
    ppermute x3, starting transfers between devices: 5.71 us -> 7.04 us  [shifted(): out.append(lax.ppermute(x, axis, [(i, (i + k) % n) for i in range(n)]))]
    pallas_call x1, Pallas kernels: 3.22 us -> 2.56 us  [local(): pl.pallas_call(functools.partial(fetch, cycles_here, fields * cycles, col...]
  transfers between devices with their start and end apart: 6 -> 6, of which waited for: 3 -> 2; matrix products, arithmetic and copies ran while one was open for 0% -> 0% of each run, Pallas kernels for 21% -> 19%
where the time goes in v5:
time: 21.1 us; the launch traced here: 20.9 us
  Pallas kernels  9.41 us (45%)
  starting transfers between devices  8.68 us (41%)
  waiting for transfers between devices  2.08 us (10%)
  between operations  0.72 us (3%)
    ppermute x3, starting transfers between devices, shifted(): out.append(lax.ppermute(x, axis, [(i, (i + k) % n) for i in range(n)]))  7.04 us
    pallas_call x1, Pallas kernels, local(): pl.pallas_call(analysis, name='analysis', out_shape=pltpu.VMEM(message, j...  3.28 us
    pallas_call x1, Pallas kernels, local(): pl.pallas_call(functools.partial(fetch, cycles_here, fields * cycles, col...  2.56 us
    pallas_call x1, Pallas kernels, local(): pl.pallas_call(functools.partial(lens, n_ord, cycles_here, fields), name=...  2.08 us
    ppermute x3, waiting for transfers between devices, swap(): return lax.ppermute(x, 'ord', [(i, i ^ k) for i in range(n_ord)])  2.07 us
    ppermute x3, starting transfers between devices, swap(): return lax.ppermute(x, 'ord', [(i, i ^ k) for i in range(n_ord)])  1.64 us
    pallas_call x1, Pallas kernels, local(): pl.pallas_call(functools.partial(near, n_ord, fields, npix_here), name='n...  0.89 us
    pallas_call x1, Pallas kernels, local(): pl.pallas_call(functools.partial(next_near, n_ord, fields, npix_here), na...  0.59 us
  transfers between devices with their start and end apart: 6, of which 2 were waited for; matrix products, arithmetic and copies ran while one was open for 0% of the time, Pallas kernels for 19%

profile of v5, /device:TPU:0, one launch (start us, length us, event | category | flops | bytes accessed | tf_op | source)
XLA Modules:
  0.0 20.9 jit_solution(7782062436832373086)
XLA Ops:
  0.6 0.0 copy-start
  0.6 0.0 copy-start.1
  0.7 3.3 %analysis.1.part_ref = f32[56,128]{1,0:T(8,128)S(1)} custom-call(s32[4]{0:T(128)} %cycle_hbm.1, s32[1,64]{1,0:T(1,128)} %bitcast.5, bf16[16,64,2048]{2,1,0:T(8,128)(2,1)} %legendre_hbm.1, bf16[6,64,2048]{2,1,0:T(8,128)(2,1)} %alm_hbm.1), custom_call_target="tpu_custom_call" | custom-call | flops 2147483648 | bytes 6291456 | tf_op jit(solution)/shard_map/analysis/pallas_call | solution.py:275
  3.9 3.1 %collective-permute-start = (f32[56,128]{1,0:T(8,128)S(1)}, f32[56,128]{1,0:T(8,128)S(1)}, u32[]{:S(2)}, u32[]{:S(2)}) collective-permute-start(f32[56,128]{1,0:T(8,128)S(1)} %analysis.1.part_ref), channel_id=1, source_target_pairs={{0,4},{4,8},{8,12},{12,0},{1,5},{5,9},{9,13},{13,1},{2,6},{6,10},{... | collective-permute-start | bytes 86024 | tf_op jit(solution)/shard_map/ppermute | solution.py:254
  7.1 2.6 %collective-permute-start.1 = (f32[56,128]{1,0:T(8,128)S(1)}, f32[56,128]{1,0:T(8,128)S(1)}, u32[]{:S(2)}, u32[]{:S(2)}) collective-permute-start(f32[56,128]{1,0:T(8,128)S(1)} %analysis.1.part_ref), channel_id=1, source_target_pairs={{0,8},{4,12},{8,0},{12,4},{1,9},{5,13},{9,1},{13,5},{2,10},{6,14},... | collective-permute-start | bytes 86024 | tf_op jit(solution)/shard_map/ppermute | solution.py:254
  9.6 1.3 %collective-permute-start.2 = (f32[56,128]{1,0:T(8,128)S(1)}, f32[56,128]{1,0:T(8,128)S(1)}, u32[]{:S(2)}, u32[]{:S(2)}) collective-permute-start(f32[56,128]{1,0:T(8,128)S(1)} %analysis.1.part_ref), channel_id=1, source_target_pairs={{0,12},{4,0},{8,4},{12,8},{1,13},{5,1},{9,5},{13,9},{2,14},{6,2},{... | collective-permute-start | bytes 86024 | tf_op jit(solution)/shard_map/ppermute | solution.py:254
  11.0 0.0 copy-done
  11.0 0.0 copy-done.1
  11.0 2.6 %fetch.1 = (f32[56,128]{1,0:T(8,128)S(1)}, s32[1,128]{1,0:T(1,128)S(1)}, bf16[128,128,128]{2,1,0:T(8,128)(2,1)S(1)}) custom-call(f32[56,128]{1,0:T(8,128)S(1)} %analysis.1.part_ref, s32[1,128]{1,0:T(1,128)S(1)} %bitcast.3, s32[1,128]{1,0:T(1,128)S(1)} %bitcast.4, bf16[128,128,128]{2,1,0:T(8,128)(2,1)} %weights_hbm.1), custom_call_target="tpu_custom_call" | custom-call | flops 1073741824 | bytes 6291456 | tf_op jit(solution)/shard_map/fetch/pallas_call | solution.py:291
  13.6 0.0 collective-permute-done
  13.6 0.0 collective-permute-done.1
  13.6 0.0 collective-permute-done.2
  13.6 0.1 collective-permute-start.5
  13.7 1.6 %collective-permute-start.3 = (f32[56,128]{1,0:T(8,128)S(1)}, f32[56,128]{1,0:T(8,128)S(1)}, u32[]{:S(2)}, u32[]{:S(2)}) collective-permute-start(f32[56,128]{1,0:T(8,128)S(1)} %add_add_fusion.refs_0_), channel_id=1, source_target_pairs={{0,2},{1,3},{2,0},{3,1},{4,6},{5,7},{6,4},{7,5},{8,10},{9,11},{10,... | collective-permute-start | bytes 86024 | tf_op jit(solution)/shard_map/ppermute | solution.py:311
  15.3 0.0 collective-permute-done.5.refs_1_
  15.3 0.9 %near.1.before_ref = f32[384,512]{1,0:T(8,128)S(1)} custom-call(f32[56,128]{1,0:T(8,128)S(1)} %add_add_fusion.refs_0_, f32[56,128]{1,0:T(8,128)S(1)} %collective-permute-done.5.refs_1_), custom_call_target="tpu_custom_call" | custom-call | flops 1073741824 | bytes 1048576 | tf_op jit(solution)/shard_map/near/pallas_call | solution.py:323
  16.2 1.5 %collective-permute-done.3.array_ref = f32[56,128]{1,0:T(8,128)S(1)} collective-permute-done((f32[56,128]{1,0:T(8,128)S(1)}, f32[56,128]{1,0:T(8,128)S(1)}, u32[]{:S(2)}, u32[]{:S(2)}) %collective-permute-start.3) | collective-permute-done | bytes 28704 | tf_op jit(solution)/shard_map/ppermute | solution.py:311
  17.6 0.0 collective-permute-start.4
  17.6 0.6 %next_near.1.refs_1_ = f32[384,512]{1,0:T(8,128)S(1)} custom-call(f32[56,128]{1,0:T(8,128)S(1)} %collective-permute-done.3.array_ref, f32[384,512]{1,0:T(8,128)S(1)} %near.1.before_ref), custom_call_target="tpu_custom_call" | custom-call | flops 1073741824 | bytes 1048576 | tf_op jit(solution)/shard_map/next_near/pallas_call | solution.py:326
  18.2 0.6 %collective-permute-done.4.refs_0_ = f32[56,128]{1,0:T(8,128)S(1)} collective-permute-done((f32[56,128]{1,0:T(8,128)S(1)}, f32[56,128]{1,0:T(8,128)S(1)}, u32[]{:S(2)}, u32[]{:S(2)}) %collective-permute-start.4) | collective-permute-done | bytes 28704 | tf_op jit(solution)/shard_map/ppermute | solution.py:311
  18.8 2.1 %lens.1 = (bf16[3,4,4096]{2,1,0:T(4,128)(2,1)}, f32[3,4,4096]{2,1,0:T(4,128)}) custom-call(s32[1,128]{1,0:T(1,128)S(1)} %get-tuple-element.5.places_vmem, f32[56,128]{1,0:T(8,128)S(1)} %collective-permute-done.4.refs_0_, f32[384,512]{1,0:T(8,128)S(1)} %next_near.1.refs_1_, bf16[128,128,128]{2,1,0:T(8,128)(2,1)S(1)} %get-tuple-element.7.refs_2_), custom_call_target="tpu_custom_call" | custom-call | tf_op jit(solution)/shard_map/lens/pallas_call | solution.py:330
  (1 shorter events, 0.0 us)
Async XLA Ops:
  0.6 10.4 %copy-start = (s32[128,1]{0,1:T(1,128)S(1)}, s32[128,1]{0,1:T(1,128)}, u32[]{:S(2)}) copy-start(s32[128,1]{0,1:T(1,128)} %param.11) | copy-start | bytes 1540
  0.6 10.4 %copy-start.1 = (s32[128]{0:T(128)S(1)}, s32[128]{0:T(128)}, u32[]{:S(2)}) copy-start(s32[128]{0:T(128)} %param.12) | copy-start | bytes 1540
  3.9 9.6 %collective-permute-start = (f32[56,128]{1,0:T(8,128)S(1)}, f32[56,128]{1,0:T(8,128)S(1)}, u32[]{:S(2)}, u32[]{:S(2)}) collective-permute-start(f32[56,128]{1,0:T(8,128)S(1)} %analysis.1.part_ref), channel_id=1, source_target_pairs={{0,4},{4,8},{8,12},{12,0},{1,5},{5,9},{9,13},{13,1},{2,6},{6,10},{... | collective-permute-start | bytes 86024 | tf_op jit(solution)/shard_map/ppermute | solution.py:254
  7.1 6.5 %collective-permute-start.1 = (f32[56,128]{1,0:T(8,128)S(1)}, f32[56,128]{1,0:T(8,128)S(1)}, u32[]{:S(2)}, u32[]{:S(2)}) collective-permute-start(f32[56,128]{1,0:T(8,128)S(1)} %analysis.1.part_ref), channel_id=1, source_target_pairs={{0,8},{4,12},{8,0},{12,4},{1,9},{5,13},{9,1},{13,5},{2,10},{6,14},... | collective-permute-start | bytes 86024 | tf_op jit(solution)/shard_map/ppermute | solution.py:254
  9.6 3.9 %collective-permute-start.2 = (f32[56,128]{1,0:T(8,128)S(1)}, f32[56,128]{1,0:T(8,128)S(1)}, u32[]{:S(2)}, u32[]{:S(2)}) collective-permute-start(f32[56,128]{1,0:T(8,128)S(1)} %analysis.1.part_ref), channel_id=1, source_target_pairs={{0,12},{4,0},{8,4},{12,8},{1,13},{5,1},{9,5},{13,9},{2,14},{6,2},{... | collective-permute-start | bytes 86024 | tf_op jit(solution)/shard_map/ppermute | solution.py:254
  13.6 1.6 %collective-permute-start.5 = (f32[56,128]{1,0:T(8,128)S(1)}, f32[56,128]{1,0:T(8,128)S(1)}, u32[]{:S(2)}, u32[]{:S(2)}) collective-permute-start(f32[56,128]{1,0:T(8,128)S(1)} %add_add_fusion.refs_0_), channel_id=1, source_target_pairs={{0,1},{1,0},{2,3},{3,2},{4,5},{5,4},{6,7},{7,6},{8,9},{9,8},{10,11... | collective-permute-start | bytes 86024 | tf_op jit(solution)/shard_map/ppermute | solution.py:311
  13.7 3.9 %collective-permute-start.3 = (f32[56,128]{1,0:T(8,128)S(1)}, f32[56,128]{1,0:T(8,128)S(1)}, u32[]{:S(2)}, u32[]{:S(2)}) collective-permute-start(f32[56,128]{1,0:T(8,128)S(1)} %add_add_fusion.refs_0_), channel_id=1, source_target_pairs={{0,2},{1,3},{2,0},{3,1},{4,6},{5,7},{6,4},{7,5},{8,10},{9,11},{10,... | collective-permute-start | bytes 86024 | tf_op jit(solution)/shard_map/ppermute | solution.py:311
  17.6 1.2 %collective-permute-start.4 = (f32[56,128]{1,0:T(8,128)S(1)}, f32[56,128]{1,0:T(8,128)S(1)}, u32[]{:S(2)}, u32[]{:S(2)}) collective-permute-start(f32[56,128]{1,0:T(8,128)S(1)} %collective-permute-done.3.array_ref), channel_id=1, source_target_pairs={{0,1},{1,0},{2,3},{3,2},{4,5},{5,4},{6,7},{7,6},{8,9},{9,8},{10,11... | collective-permute-start | bytes 86024 | tf_op jit(solution)/shard_map/ppermute | solution.py:311

commit v6 on v5

--- a/solution.py
+++ b/solution.py
@@ -99,11 +99,13 @@
         out_ref[f * cycles : (f + 1) * cycles, :] = jnp.concatenate(pieces, axis=1)
 
 
-def fetch(cycles_here, rows_col, cols, part_ref, src_band_ref, src_block_ref, weights_hbm, part_out, places_ref, weights_ref, stage, sems):
-    count = weights_ref.shape[0] // CHUNKS
+def fetch(cycles_here, rows_col, cols, part_ref, src_band_ref, src_block_ref, weights_hbm, part_out, places_ref, weights_ref, rest_ref, stage, sems):
+    count = rest_ref.shape[0]
     copies = [
         pltpu.make_async_copy(
-            weights_hbm.at[pl.ds(i * count, count)], stage.at[pl.ds(i * count, count)], sems.at[i]
+            weights_hbm.at[pl.ds(i * count, count)],
+            stage.at[pl.ds(i * count, count)] if i < CHUNKS - 1 else rest_ref,
+            sems.at[i],
         )
         for i in range(CHUNKS)
     ]
@@ -113,13 +115,15 @@
     block = src_block_ref[...]
     cycle = src_band_ref[...] * cycles_here + lax.shift_right_logical(block, cols.bit_length() - 1)
     places_ref[...] = (block & (cols - 1)) * rows_col + cycle
-    for i, copy in enumerate(copies):
+    for i, copy in enumerate(copies[:-1]):
         copy.wait()
 
         @pl.loop(0, count, step=UNROLL)
         def _(k):
             for j in range(UNROLL):
                 weights_ref[i * count + k + j] = stage[i * count + k + j].T
+
+    copies[-1].wait()
 
 
 def synthesis(n_ord, fields, npix_here, arrays):
@@ -173,7 +177,13 @@
 
 
 def near(n_ord, fields, npix_here, *refs):
-    refs[-1][...] = synthesis(n_ord, fields, npix_here, [r[...] for r in refs[:-1]])
+    rest, out, turned = refs[-3:]
+    out[...] = synthesis(n_ord, fields, npix_here, [r[...] for r in refs[:-3]])
+
+    @pl.loop(0, rest.shape[0], step=UNROLL)
+    def _(k):
+        for j in range(UNROLL):
+            turned[k + j] = rest[k + j].T
 
 
 def next_near(n_ord, fields, npix_here, array_ref, before_ref, out_ref):
@@ -183,9 +193,11 @@
 def lens(n_ord, cycles_here, fields, places_vmem, *refs):
     last = n_ord // 2 - 1
     arrays = refs[:last]
-    near_ref, weights, sky_hbm, lensed_hbm, sky, stage, sky_out, lensed_out, places, sems = refs[last:]
+    near_ref, weights_a, weights_b, sky_hbm, lensed_hbm, sky, stage, sky_out, lensed_out, places, sems = refs[last:]
     listing = pltpu.make_async_copy(places_vmem, places, sems.at[CHUNKS + 1])
     listing.start()
+    stage[...] = jnp.zeros_like(stage)
+    weights = [w.at[i] for w in (weights_a, weights_b) for i in range(w.shape[0])]
     band = lax.axis_index("band")
     cycles = (arrays[0].shape[0] - META) // fields
     npix_here = sky_out.shape[2]
@@ -212,7 +224,6 @@
     copies[0].start()
 
     listing.wait()
-    stage[...] = jnp.zeros_like(stage)
     for col in range(cols):
         for c in range(cycles_here):
             source = sky[pl.ds(places[0, c * cols + col], fields, stride=cycles), :]
@@ -225,7 +236,7 @@
         left = jnp.concatenate([stage[2 * col], stage[2 * col + 1]], axis=1).astype(jnp.bfloat16)
         right = jnp.concatenate(
             [
-                jnp.concatenate([weights[c * cols + col] for c in range(n, cycles_here, 2)], axis=1)
+                jnp.concatenate([weights[c * cols + col][...] for c in range(n, cycles_here, 2)], axis=1)
                 for n in range(2)
             ],
             axis=0,
@@ -288,17 +299,20 @@
         compiler_params=pltpu.CompilerParams(vmem_limit_bytes=16 << 20),
         cost_estimate=pl.CostEstimate(flops=2 << 30, bytes_accessed=6 << 20, transcendentals=0),
     )(*far(cycle_number, order_ids[None], legendre, alm))
-    own, places, weights = pl.pallas_call(
+    few = (blocks // CHUNKS, blk, blk)
+    most = (blocks - few[0], blk, blk)
+    own, places, weights_a, weights_b = pl.pallas_call(
         functools.partial(fetch, cycles_here, fields * cycles, cols),
         name="fetch",
         out_shape=(
             pltpu.VMEM(part.shape, part.dtype),
             pltpu.VMEM((1, blocks), jnp.int32),
-            pltpu.VMEM(weights.shape, weights.dtype),
+            pltpu.VMEM(most, weights.dtype),
+            pltpu.VMEM(few, weights.dtype),
         ),
         in_specs=[vmem, vmem, vmem, hbm],
-        out_specs=(vmem, vmem, vmem),
-        scratch_shapes=[pltpu.VMEM(weights.shape, weights.dtype), pltpu.SemaphoreType.DMA((CHUNKS,))],
+        out_specs=(vmem,) * 4,
+        scratch_shapes=[pltpu.VMEM(most, weights.dtype), pltpu.SemaphoreType.DMA((CHUNKS,))],
         compiler_params=pltpu.CompilerParams(vmem_limit_bytes=16 << 20),
         cost_estimate=pl.CostEstimate(flops=1 << 30, bytes_accessed=6 << 20, transcendentals=0),
     )(part, src_band.T, src_block[None], *far(weights))
@@ -315,23 +329,32 @@
     there = swap(total, half)
     rest = [swap(there, k) for k in range(1, half)]
     synth = dict(
-        out_shape=pltpu.VMEM((npix_here // q_len * fields * cycles, q_len), jnp.float32),
-        out_specs=vmem,
         compiler_params=pltpu.CompilerParams(vmem_limit_bytes=16 << 20),
         cost_estimate=pl.CostEstimate(flops=1 << 30, bytes_accessed=1 << 20, transcendentals=0),
     )
+    partial_sky = pltpu.VMEM((npix_here // q_len * fields * cycles, q_len), jnp.float32)
+    sums, weights_b = pl.pallas_call(
+        functools.partial(near, n_ord, fields, npix_here),
+        name="near",
+        in_specs=[vmem] * (half + 1),
+        out_shape=(partial_sky, pltpu.VMEM(few, weights.dtype)),
+        out_specs=(vmem, vmem),
+        **synth,
+    )(*here, weights_b)
     sums = pl.pallas_call(
-        functools.partial(near, n_ord, fields, npix_here), name="near", in_specs=[vmem] * half, **synth
-    )(*here)
-    sums = pl.pallas_call(
-        functools.partial(next_near, n_ord, fields, npix_here), name="next_near", in_specs=[vmem] * 2, **synth
+        functools.partial(next_near, n_ord, fields, npix_here),
+        name="next_near",
+        in_specs=[vmem] * 2,
+        out_shape=partial_sky,
+        out_specs=vmem,
+        **synth,
     )(there, sums)
     pixels = (fields, cycles_here, npix_here)
     return pl.pallas_call(
         functools.partial(lens, n_ord, cycles_here, fields),
         name="lens",
         out_shape=(jax.ShapeDtypeStruct(pixels, jnp.bfloat16), jax.ShapeDtypeStruct(pixels, jnp.float32)),
-        in_specs=[vmem] * (half + 2),
+        in_specs=[vmem] * (half + 3),
         out_specs=(hbm, hbm),
         scratch_shapes=[
             pltpu.VMEM((cols * fields * cycles, blk), jnp.float32),
@@ -342,7 +365,7 @@
             pltpu.SemaphoreType.DMA((CHUNKS + 2,)),
         ],
         compiler_params=pltpu.CompilerParams(vmem_limit_bytes=32 << 20),
-    )(places, *rest, sums, weights)
+    )(places, *rest, sums, weights_a, weights_b)
 
 
 def solution(mesh):

time: 21.1 us -> 21.2 us (level)
  waiting for transfers between devices: 2.08 us -> 2.63 us
  Pallas kernels: 9.41 us -> 9.1 us
    pallas_call x1, Pallas kernels: 2.56 us -> 2.24 us  [local(): pl.pallas_call(functools.partial(fetch, cycles_here, fields * cycles, col...]
    ppermute x3, waiting for transfers between devices: 2.07 us -> 2.38 us  [swap(): return lax.ppermute(x, 'ord', [(i, i ^ k) for i in range(n_ord)])]
    ppermute x3, waiting for transfers between devices: 0.01 us -> 0.26 us  [shifted(): out.append(lax.ppermute(x, axis, [(i, (i + k) % n) for i in range(n)]))]
  transfers between devices with their start and end apart: 6 -> 6, of which waited for: 2 -> 2; matrix products, arithmetic and copies ran while one was open for 0% -> 0% of each run, Pallas kernels for 19% -> 18%
where the time goes in v6:
time: 21.2 us; the launch traced here: 21.1 us
  Pallas kernels  9.1 us (43%)
  starting transfers between devices  8.61 us (41%)
  waiting for transfers between devices  2.63 us (12%)
  between operations  0.71 us (3%)
    ppermute x3, starting transfers between devices, shifted(): out.append(lax.ppermute(x, axis, [(i, (i + k) % n) for i in range(n)]))  7.04 us
    pallas_call x1, Pallas kernels, local(): pl.pallas_call(analysis, name='analysis', out_shape=pltpu.VMEM(message, j...  3.28 us
    ppermute x3, waiting for transfers between devices, swap(): return lax.ppermute(x, 'ord', [(i, i ^ k) for i in range(n_ord)])  2.38 us
    pallas_call x1, Pallas kernels, local(): pl.pallas_call(functools.partial(fetch, cycles_here, fields * cycles, col...  2.24 us
    pallas_call x1, Pallas kernels, local(): pl.pallas_call(functools.partial(lens, n_ord, cycles_here, fields), name=...  2.08 us
    ppermute x3, starting transfers between devices, swap(): return lax.ppermute(x, 'ord', [(i, i ^ k) for i in range(n_ord)])  1.57 us
    pallas_call x1, Pallas kernels, local(): pl.pallas_call(functools.partial(near, n_ord, fields, npix_here), name='n...  0.91 us
    pallas_call x1, Pallas kernels, local(): pl.pallas_call(functools.partial(next_near, n_ord, fields, npix_here), na...  0.59 us
  transfers between devices with their start and end apart: 6, of which 2 were waited for; matrix products, arithmetic and copies ran while one was open for 0% of the time, Pallas kernels for 18%

profile of v6, /device:TPU:0, one launch (start us, length us, event | category | flops | bytes accessed | tf_op | source)
XLA Modules:
  0.0 21.1 jit_solution(7882712597597108801)
XLA Ops:
  0.6 0.0 copy-start
  0.6 0.0 copy-start.1
  0.7 3.3 %analysis.1.part_ref = f32[56,128]{1,0:T(8,128)S(1)} custom-call(s32[4]{0:T(128)} %cycle_hbm.1, s32[1,64]{1,0:T(1,128)} %bitcast.5, bf16[16,64,2048]{2,1,0:T(8,128)(2,1)} %legendre_hbm.1, bf16[6,64,2048]{2,1,0:T(8,128)(2,1)} %alm_hbm.1), custom_call_target="tpu_custom_call" | custom-call | flops 2147483648 | bytes 6291456 | tf_op jit(solution)/shard_map/analysis/pallas_call | solution.py:286
  3.9 3.1 %collective-permute-start = (f32[56,128]{1,0:T(8,128)S(1)}, f32[56,128]{1,0:T(8,128)S(1)}, u32[]{:S(2)}, u32[]{:S(2)}) collective-permute-start(f32[56,128]{1,0:T(8,128)S(1)} %analysis.1.part_ref), channel_id=1, source_target_pairs={{0,4},{4,8},{8,12},{12,0},{1,5},{5,9},{9,13},{13,1},{2,6},{6,10},{... | collective-permute-start | bytes 86024 | tf_op jit(solution)/shard_map/ppermute | solution.py:265
  7.1 2.6 %collective-permute-start.1 = (f32[56,128]{1,0:T(8,128)S(1)}, f32[56,128]{1,0:T(8,128)S(1)}, u32[]{:S(2)}, u32[]{:S(2)}) collective-permute-start(f32[56,128]{1,0:T(8,128)S(1)} %analysis.1.part_ref), channel_id=1, source_target_pairs={{0,8},{4,12},{8,0},{12,4},{1,9},{5,13},{9,1},{13,5},{2,10},{6,14},... | collective-permute-start | bytes 86024 | tf_op jit(solution)/shard_map/ppermute | solution.py:265
  9.6 1.3 %collective-permute-start.2 = (f32[56,128]{1,0:T(8,128)S(1)}, f32[56,128]{1,0:T(8,128)S(1)}, u32[]{:S(2)}, u32[]{:S(2)}) collective-permute-start(f32[56,128]{1,0:T(8,128)S(1)} %analysis.1.part_ref), channel_id=1, source_target_pairs={{0,12},{4,0},{8,4},{12,8},{1,13},{5,1},{9,5},{13,9},{2,14},{6,2},{... | collective-permute-start | bytes 86024 | tf_op jit(solution)/shard_map/ppermute | solution.py:265
  11.0 0.0 copy-done
  11.0 0.0 copy-done.1
  11.0 2.2 %fetch.1 = (f32[56,128]{1,0:T(8,128)S(1)}, s32[1,128]{1,0:T(1,128)S(1)}, bf16[96,128,128]{2,1,0:T(8,128)(2,1)S(1)}, bf16[32,128,128]{2,1,0:T(8,128)(2,1)S(1)}) custom-call(f32[56,128]{1,0:T(8,128)S(1)} %analysis.1.part_ref, s32[1,128]{1,0:T(1,128)S(1)} %bitcast.3, s32[1,128]{1,0:T(1,128)S(1)} %bitcast.4, bf16[128,128,128]{2,1,0:T(8,128)(2,1)} %weights_hbm.1), custom_call_target="tpu_custom_call" | custom-call | flops 1073741824 | bytes 6291456 | tf_op jit(solution)/shard_map/fetch/pallas_call | solution.py:304
  13.2 0.0 collective-permute-done
  13.2 0.0 collective-permute-done.1
  13.3 0.3 %collective-permute-done.2 = f32[56,128]{1,0:T(8,128)S(1)} collective-permute-done((f32[56,128]{1,0:T(8,128)S(1)}, f32[56,128]{1,0:T(8,128)S(1)}, u32[]{:S(2)}, u32[]{:S(2)}) %collective-permute-start.2) | collective-permute-done | bytes 28704 | tf_op jit(solution)/shard_map/ppermute | solution.py:265
  13.5 1.6 %collective-permute-start.3 = (f32[56,128]{1,0:T(8,128)S(1)}, f32[56,128]{1,0:T(8,128)S(1)}, u32[]{:S(2)}, u32[]{:S(2)}) collective-permute-start(f32[56,128]{1,0:T(8,128)S(1)} %add_add_fusion.refs_0_), channel_id=1, source_target_pairs={{0,2},{1,3},{2,0},{3,1},{4,6},{5,7},{6,4},{7,5},{8,10},{9,11},{10,... | collective-permute-start | bytes 86024 | tf_op jit(solution)/shard_map/ppermute | solution.py:325
  15.1 0.0 collective-permute-start.5
  15.1 2.4 %collective-permute-done.3.array_ref = f32[56,128]{1,0:T(8,128)S(1)} collective-permute-done((f32[56,128]{1,0:T(8,128)S(1)}, f32[56,128]{1,0:T(8,128)S(1)}, u32[]{:S(2)}, u32[]{:S(2)}) %collective-permute-start.3) | collective-permute-done | bytes 28704 | tf_op jit(solution)/shard_map/ppermute | solution.py:325
  17.5 0.0 collective-permute-start.4
  17.5 0.0 collective-permute-done.5.refs_1_
  17.5 0.9 %near.1 = (f32[384,512]{1,0:T(8,128)S(1)}, bf16[32,128,128]{2,1,0:T(8,128)(2,1)S(1)}) custom-call(f32[56,128]{1,0:T(8,128)S(1)} %add_add_fusion.refs_0_, f32[56,128]{1,0:T(8,128)S(1)} %collective-permute-done.5.refs_1_, bf16[32,128,128]{2,1,0:T(8,128)(2,1)S(1)} %get-tuple-element.10.refs_2_), custom_call_target="tpu_custom_call" | custom-call | flops 1073741824 | bytes 1048576 | tf_op jit(solution)/shard_map/near/pallas_call | solution.py:336
  18.4 0.6 %next_near.1.refs_1_ = f32[384,512]{1,0:T(8,128)S(1)} custom-call(f32[56,128]{1,0:T(8,128)S(1)} %collective-permute-done.3.array_ref, f32[384,512]{1,0:T(8,128)S(1)} %get-tuple-element.11.before_ref), custom_call_target="tpu_custom_call" | custom-call | flops 1073741824 | bytes 1048576 | tf_op jit(solution)/shard_map/next_near/pallas_call | solution.py:344
  19.0 0.0 collective-permute-done.4.refs_0_
  19.0 2.1 %lens.1 = (bf16[3,4,4096]{2,1,0:T(4,128)(2,1)}, f32[3,4,4096]{2,1,0:T(4,128)}) custom-call(s32[1,128]{1,0:T(1,128)S(1)} %get-tuple-element.8.places_vmem, f32[56,128]{1,0:T(8,128)S(1)} %collective-permute-done.4.refs_0_, f32[384,512]{1,0:T(8,128)S(1)} %next_near.1.refs_1_, bf16[96,128,128]{2,1,0:T(8,128)(2,1)S(1)} %get-tuple-element.12.refs_2_, ...), custom_call_target="tpu_custom_call" | custom-call | tf_op jit(solution)/shard_map/lens/pallas_call | solution.py:353
  (1 shorter events, 0.0 us)
Async XLA Ops:
  0.6 10.4 %copy-start = (s32[128,1]{0,1:T(1,128)S(1)}, s32[128,1]{0,1:T(1,128)}, u32[]{:S(2)}) copy-start(s32[128,1]{0,1:T(1,128)} %param.11) | copy-start | bytes 1540
  0.6 10.4 %copy-start.1 = (s32[128]{0:T(128)S(1)}, s32[128]{0:T(128)}, u32[]{:S(2)}) copy-start(s32[128]{0:T(128)} %param.12) | copy-start | bytes 1540
  3.9 9.3 %collective-permute-start = (f32[56,128]{1,0:T(8,128)S(1)}, f32[56,128]{1,0:T(8,128)S(1)}, u32[]{:S(2)}, u32[]{:S(2)}) collective-permute-start(f32[56,128]{1,0:T(8,128)S(1)} %analysis.1.part_ref), channel_id=1, source_target_pairs={{0,4},{4,8},{8,12},{12,0},{1,5},{5,9},{9,13},{13,1},{2,6},{6,10},{... | collective-permute-start | bytes 86024 | tf_op jit(solution)/shard_map/ppermute | solution.py:265
  7.1 6.2 %collective-permute-start.1 = (f32[56,128]{1,0:T(8,128)S(1)}, f32[56,128]{1,0:T(8,128)S(1)}, u32[]{:S(2)}, u32[]{:S(2)}) collective-permute-start(f32[56,128]{1,0:T(8,128)S(1)} %analysis.1.part_ref), channel_id=1, source_target_pairs={{0,8},{4,12},{8,0},{12,4},{1,9},{5,13},{9,1},{13,5},{2,10},{6,14},... | collective-permute-start | bytes 86024 | tf_op jit(solution)/shard_map/ppermute | solution.py:265
  9.6 3.9 %collective-permute-start.2 = (f32[56,128]{1,0:T(8,128)S(1)}, f32[56,128]{1,0:T(8,128)S(1)}, u32[]{:S(2)}, u32[]{:S(2)}) collective-permute-start(f32[56,128]{1,0:T(8,128)S(1)} %analysis.1.part_ref), channel_id=1, source_target_pairs={{0,12},{4,0},{8,4},{12,8},{1,13},{5,1},{9,5},{13,9},{2,14},{6,2},{... | collective-permute-start | bytes 86024 | tf_op jit(solution)/shard_map/ppermute | solution.py:265
  13.5 3.9 %collective-permute-start.3 = (f32[56,128]{1,0:T(8,128)S(1)}, f32[56,128]{1,0:T(8,128)S(1)}, u32[]{:S(2)}, u32[]{:S(2)}) collective-permute-start(f32[56,128]{1,0:T(8,128)S(1)} %add_add_fusion.refs_0_), channel_id=1, source_target_pairs={{0,2},{1,3},{2,0},{3,1},{4,6},{5,7},{6,4},{7,5},{8,10},{9,11},{10,... | collective-permute-start | bytes 86024 | tf_op jit(solution)/shard_map/ppermute | solution.py:325
  15.1 2.4 %collective-permute-start.5 = (f32[56,128]{1,0:T(8,128)S(1)}, f32[56,128]{1,0:T(8,128)S(1)}, u32[]{:S(2)}, u32[]{:S(2)}) collective-permute-start(f32[56,128]{1,0:T(8,128)S(1)} %add_add_fusion.refs_0_), channel_id=1, source_target_pairs={{0,1},{1,0},{2,3},{3,2},{4,5},{5,4},{6,7},{7,6},{8,9},{9,8},{10,11... | collective-permute-start | bytes 86024 | tf_op jit(solution)/shard_map/ppermute | solution.py:325
  17.5 1.5 %collective-permute-start.4 = (f32[56,128]{1,0:T(8,128)S(1)}, f32[56,128]{1,0:T(8,128)S(1)}, u32[]{:S(2)}, u32[]{:S(2)}) collective-permute-start(f32[56,128]{1,0:T(8,128)S(1)} %collective-permute-done.3.array_ref), channel_id=1, source_target_pairs={{0,1},{1,0},{2,3},{3,2},{4,5},{5,4},{6,7},{7,6},{8,9},{9,8},{10,11... | collective-permute-start | bytes 86024 | tf_op jit(solution)/shard_map/ppermute | solution.py:325
